TPU v7x, 16 devices: a 4x2x1 block of a 4x4x8 slice. The times are simulated.
16 devices in a mesh: dp: 2 (over y, z), tp: 8 (over x, core).
Axes of the slice: x: 4, y: 2, z: 1, core: 2. Of those that a mesh axis runs over, the one named last changes fastest.
The devices are a block of a 4x4x8 slice.
Arguments:
- x_in: bfloat16 [256, 7168], P('dp'), parts along dimension 0
- pos_ids: int32 [256], P('dp'), parts along dimension 0
- ckv_cache: bfloat16 [2, 256, 128, 512], P(None, 'dp'), parts along dimension 1
- kpe_cache: bfloat16 [2, 256, 128, 64], P(None, 'dp'), parts along dimension 1
- attn_gain: bfloat16 [2, 7168], replicated
- w_dq: bfloat16 [2, 7168, 1536], replicated
- q_gain: bfloat16 [2, 1536], replicated
- w_dkv: bfloat16 [2, 7168, 576], replicated
- kv_gain: bfloat16 [2, 512], replicated
- w_uq: bfloat16 [2, 1536, 32, 192], P(None, None, 'tp')
- w_uk: bfloat16 [2, 512, 32, 128], P(None, None, 'tp')
- w_uv: bfloat16 [2, 512, 32, 128], P(None, None, 'tp')
- w_o: bfloat16 [2, 32, 128, 7168], P(None, 'tp')
- mlp_gain: bfloat16 [2, 7168], replicated
- w_gate: bfloat16 [2, 7168, 4608], P(None, None, 'tp')
- w_up: bfloat16 [2, 7168, 4608], P(None, None, 'tp')
- w_down: bfloat16 [2, 4608, 7168], P(None, 'tp')
Outputs:
- output 1: bfloat16 [256, 7168], P('dp'), parts along dimension 0
- output 2: bfloat16 [2, 256, 512], P(None, 'dp'), parts along dimension 1
- output 3: bfloat16 [2, 256, 64], P(None, 'dp'), parts along dimension 1
There are 2 independent parts. A program takes and returns all parts, laid end to end along the dimension named above; an argument that names none is the same for every part.
All inputs are finite; a program needn't handle non-finite values.
Results may differ from a plain program's by a relative error of at most 0.02.
Values are sent between devices in bfloat16 or wider.
A program may use at most 768 MiB of HBM per device.

v0:
```python
import math
import jax
import jax.numpy as jnp
from jax import lax
from jax.sharding import PartitionSpec as P

NORM_EPS = 1e-6
ROPE_BASE = 10000.0


def rms_norm(values, norm_gain):
    values = values.astype(jnp.float32)
    inv_rms = lax.rsqrt(jnp.mean(values * values, axis=-1, keepdims=True) + NORM_EPS)
    return (values * inv_rms * norm_gain.astype(jnp.float32)).astype(jnp.bfloat16)


def rotary(values, positions):
    half_dim = values.shape[-1] // 2
    inv_freq = jnp.exp(jnp.arange(half_dim, dtype=jnp.float32) * (-2.0 * math.log(ROPE_BASE) / values.shape[-1]))
    angles = positions.astype(jnp.float32)[..., None] * inv_freq
    cos_part = jnp.cos(angles)
    sin_part = jnp.sin(angles)
    lo_half = values[..., :half_dim]
    hi_half = values[..., half_dim:]
    return jnp.concatenate([lo_half * cos_part - hi_half * sin_part, hi_half * cos_part + lo_half * sin_part], axis=-1)


def latent_attention(q_lat, q_rope, ckv_old, kpe_old, ckv_new, kpe_new, positions, score_scale):
    scores = jnp.einsum('bhc,btc->bht', q_lat, ckv_old, preferred_element_type=jnp.float32)
    scores = scores + jnp.einsum('bhr,btr->bht', q_rope, kpe_old, preferred_element_type=jnp.float32)
    fresh_score = jnp.einsum('bhc,bc->bh', q_lat, ckv_new, preferred_element_type=jnp.float32)
    fresh_score = fresh_score + jnp.einsum('bhr,br->bh', q_rope, kpe_new, preferred_element_type=jnp.float32)
    key_steps = jnp.arange(ckv_old.shape[1])[None, None, :]
    pos_limit = positions[:, None, None]
    at_pos = key_steps == pos_limit
    scores = jnp.where(at_pos, fresh_score[:, :, None], scores) * score_scale
    scores = jnp.where(key_steps <= pos_limit, scores, -jnp.inf)
    attn_prob = jax.nn.softmax(scores, axis=-1).astype(jnp.bfloat16)
    bf_zero = jnp.zeros((), jnp.bfloat16)
    new_prob = jnp.sum(jnp.where(at_pos, attn_prob, bf_zero), axis=-1).astype(jnp.float32)
    context = jnp.einsum('bht,btc->bhc', jnp.where(at_pos, bf_zero, attn_prob), ckv_old, preferred_element_type=jnp.float32)
    context = context + new_prob[:, :, None] * ckv_new.astype(jnp.float32)[:, None, :]
    return context.astype(jnp.bfloat16)


def attention_heads(normed, positions, ckv_old, kpe_old, w_dq, q_gain, w_dkv, kv_gain, w_uq, w_uk, w_uv):
    value_a8 = ckv_old.shape[-1]
    nope_dim = w_uk.shape[-1]
    c_q = rms_norm(jnp.dot(normed, w_dq, preferred_element_type=jnp.float32), q_gain)
    q_full = jnp.einsum('bc,chd->bhd', c_q, w_uq, preferred_element_type=jnp.float32)
    q_nope = q_full[..., :nope_dim].astype(jnp.bfloat16)
    q_rope = rotary(q_full[..., nope_dim:], positions[:, None]).astype(jnp.bfloat16)
    q_lat = jnp.einsum('bhn,chn->bhc', q_nope, w_uk, preferred_element_type=jnp.float32).astype(jnp.bfloat16)
    kv_lat = jnp.dot(normed, w_dkv, preferred_element_type=jnp.float32)
    ckv_new = rms_norm(kv_lat[:, :value_a8], kv_gain)
    kpe_new = rotary(kv_lat[:, value_a8:], positions).astype(jnp.bfloat16)
    context = latent_attention(q_lat, q_rope, ckv_old, kpe_old, ckv_new, kpe_new, positions, w_uq.shape[-1] ** -0.5)
    head_out = jnp.einsum('bhc,chv->bhv', context, w_uv, preferred_element_type=jnp.float32).astype(jnp.bfloat16)
    return head_out, ckv_new, kpe_new


def gated_mlp(mlp_in, w_gate, w_up, w_down):
    gate_pre = jnp.dot(mlp_in, w_gate, preferred_element_type=jnp.float32)
    up_pre = jnp.dot(mlp_in, w_up, preferred_element_type=jnp.float32)
    act_out = (jax.nn.silu(gate_pre) * up_pre).astype(jnp.bfloat16)
    return jnp.dot(act_out, w_down, preferred_element_type=jnp.float32)


def local_layer(hidden, positions, ckv_old, kpe_old, weights):
    (attn_gain, w_dq, q_gain, w_dkv, kv_gain, w_uq, w_uk, w_uv, w_o, mlp_gain, w_gate, w_up, w_down) = weights
    normed = rms_norm(hidden, attn_gain)
    head_out, ckv_new, kpe_new = attention_heads(normed, positions, ckv_old, kpe_old, w_dq, q_gain, w_dkv, kv_gain, w_uq, w_uk, w_uv)
    attn_part = jnp.einsum('bhv,hvd->bd', head_out, w_o, preferred_element_type=jnp.float32).astype(jnp.bfloat16)
    attn_sum = lax.psum(attn_part, 'tp')
    mid_state = (hidden.astype(jnp.float32) + attn_sum.astype(jnp.float32)).astype(jnp.bfloat16)
    mlp_part = gated_mlp(rms_norm(mid_state, mlp_gain), w_gate, w_up, w_down).astype(jnp.bfloat16)
    mlp_sum = lax.psum(mlp_part, 'tp')
    layer_out = (mid_state.astype(jnp.float32) + mlp_sum.astype(jnp.float32)).astype(jnp.bfloat16)
    return layer_out, ckv_new, kpe_new


def solution(mesh):
    cache_spec = P(None, 'dp', None, None)
    head_spec = P(None, None, 'tp', None)
    weight_specs = (P(), P(), P(), P(), P(), head_spec, head_spec, head_spec, P(None, 'tp', None, None), P(), P(None, None, 'tp'), P(None, None, 'tp'), P(None, 'tp', None))
    in_specs = (P('dp', None), P('dp'), cache_spec, cache_spec) + weight_specs
    out_specs = (P('dp', None), P(None, 'dp', None), P(None, 'dp', None))

    def device_body(x_in, pos_ids, ckv_cache, kpe_cache, *params):
        hidden = x_in
        c_rows = []
        k_rows = []
        for layer_idx in range(ckv_cache.shape[0]):
            weights = [weight[layer_idx] for weight in params]
            hidden, c_row, k_row = local_layer(hidden, pos_ids, ckv_cache[layer_idx], kpe_cache[layer_idx], weights)
            c_rows.append(c_row)
            k_rows.append(k_row)
        return hidden, jnp.stack(c_rows), jnp.stack(k_rows)

    return jax.shard_map(device_body, mesh=mesh, in_specs=in_specs, out_specs=out_specs, check_vma=False)
```

profile of v0, /device:TPU:113, one launch (start us, length us, event | category | flops | bytes accessed | tf_op | source)
XLA Modules:
  0.0 415.2 jit_solution(316000889970724592)
XLA Ops:
  7.3 0.7 convert_element_type.191
  7.9 0.7 iota_compare_fusion
  8.7 1.9 fusion.48
  10.6 1.4 slice_convert_fusion.8
  12.0 1.5 slice_convert_fusion.5
  13.5 6.4 %fusion.34 = f32[128,576]{0,1:T(8,128)S(1)} fusion(bf16[2,7168,576]{1,2,0:T(8,128)(2,1)} %param.24, bf16[128,7168]{1,0:T(8,128)(2,1)} %param.17, f32[7168]{0:T(1024)S(1)} %bitcast.198, f32[128]{0:T(128)S(1)} %add_rsqrt_fusion.7), kind=kOutput, calls=%fused_computation.38 | convolution fusion | flops 1060634624 | bytes 10416640 | tf_op jit(solution)/shard_map/dot_general | solution.py:54
  20.3 0.6 convert_reduce_fusion
  21.1 0.7 copy.34
  21.8 0.2 copy.32
  22.0 0.8 copy.24
  22.8 9.6 %multiply_reduce_fusion.1 = (f32[128]{0:T(128)S(1)}, f32[128,1536]{1,0:T(8,128)S(1)}) fusion(bf16[2,7168,1536]{2,1,0:T(8,128)(2,1)} %param.22, bf16[128,7168]{1,0:T(8,128)(2,1)S(1)} %copy-done, f32[7168]{0:T(1024)S(1)} %bitcast.199, f32[128]{0:T(128)S(1)} %add_rsqrt_fusion.7), kind=kOutput, calls=%fused_computation.117 | convolution fusion | flops 2822635520 | bytes 24671232 | tf_op jit(solution)/shard_map/dot_general | solution.py:49
  32.5 0.4 fusion.202
  32.9 1.3 slice_bitcast_fusion.1
  34.2 2.8 fusion.201
  37.1 0.8 fusion.154
  37.9 0.4 fusion.82
  38.3 0.4 copy-done.6
  38.7 0.8 copy-done.9
  39.5 1.3 fusion.151
  40.8 11.1 %fusion.14 = f32[128,4,128]{2,1,0:T(4,128)} fusion(bf16[2,128,128,512]{3,2,1,0:T(8,128)(2,1)} %param.19, bf16[128,4,512]{2,0,1:T(8,128)(2,1)} %copy-done.9), kind=kOutput, calls=%fused_computation.14 | convolution fusion | flops 67108864 | bytes 17563648 | tf_op jit(solution)/shard_map/bhc,btc->bht/dot_general | solution.py:29
  51.9 0.9 subtract_convert_fusion.1
  53.0 1.2 fusion.209
  54.2 0.6 add.126
  54.8 3.1 fusion.203
  57.9 1.2 select_reduce_fusion.1
  59.1 8.9 %fusion.73 = bf16[128,4,512]{2,1,0:T(4,128)(2,1)} fusion(bf16[2,128,128,512]{3,2,1,0:T(8,128)(2,1)} %param.19, f32[128,512]{1,0:T(8,128)} %copy.24, f32[128,4]{1,0:T(8,128)S(1)} %convert_element_type.193, bf16[128,4,128]{2,1,0:T(4,128)(2,1)S(1)} %get-tuple-element.17, pred[128,128]{1,0:T(8,128)(4,1)S(1)} %get-tuple-element.41), kind=kOutput, calls=%fused_computation.89 | convolution fusion | flops 67960832 | bytes 17713152 | tf_op jit(solution)/shard_map/bht,btc->bhc/dot_general | solution.py:41
  67.9 6.0 %fusion.20 = bf16[128,7168]{1,0:T(8,128)(2,1)} fusion(bf16[2,4,128,7168]{3,2,1,0:T(8,128)(2,1)} %param.29, bf16[512,4,128]{2,1,0:T(4,128)(2,1)} %get-tuple-element.22, bf16[128,4,512]{2,1,0:T(4,128)(2,1)} %fusion.73), kind=kOutput, calls=%fused_computation.22 | convolution fusion | flops 1007616000 | bytes 10223616 | tf_op jit(solution)/shard_map/bhv,hvd->bd/dot_general | solution.py:73
  74.0 0.2 all-reduce.7.cloned.1.call-start
  74.3 0.6 slice_convert_fusion.4
  74.9 56.8 %all-reduce.5.cloned.1.call-done = bf16[128,7168]{1,0:T(8,128)(2,1)} async-done(((bf16[128,7168]{1,0:T(8,128)(2,1)}), bf16[128,7168]{1,0:T(8,128)(2,1)}) %all-reduce.5.cloned.1.call-update) | async-done | bytes 1835024 | tf_op jit(solution)/shard_map/psum | solution.py:74
  131.7 2.8 fusion.52
  134.5 1.2 copy-done.3
  135.8 6.4 %fusion.32 = f32[128,576]{0,1:T(8,128)} fusion(bf16[2,7168,576]{1,2,0:T(8,128)(2,1)} %param.31, bf16[128,7168]{1,0:T(8,128)(2,1)S(1)} %get-tuple-element.15, f32[7168]{0:T(1024)S(1)} %bitcast.200, f32[128]{0:T(128)S(1)} %add_rsqrt_fusion.4), kind=kOutput, calls=%fused_computation.36 | convolution fusion | flops 1060634624 | bytes 10416640 | tf_op jit(solution)/shard_map/dot_general | solution.py:63
  142.2 14.3 %convolution_convert_fusion.1 = bf16[128,7168]{1,0:T(8,128)(2,1)} fusion(bf16[2,576,7168]{2,1,0:T(8,128)(2,1)} %param.33, bf16[2,7168,576]{1,2,0:T(8,128)(2,1)} %param.32, bf16[128,7168]{1,0:T(8,128)(2,1)} %copy-done.3, f32[7168]{0:T(1024)S(1)} %bitcast.201, f32[128]{0:T(128)S(1)} %add_rsqrt_fusion.4, f32[128,576]{0,1:T(8,128)} %fusion.32), kind=kOutput, calls=%fused_computation.25 | convolution fusion | flops 2118959104 | bytes 20509184 | tf_op jit(solution)/shard_map/dot_general | solution.py:66
  156.6 56.1 %all-reduce.7.cloned.1.call-done = bf16[128,7168]{1,0:T(8,128)(2,1)} async-done(((bf16[128,7168]{1,0:T(8,128)(2,1)}), bf16[128,7168]{1,0:T(8,128)(2,1)}) %all-reduce.7.cloned.1.call-update) | async-done | bytes 1835024 | tf_op jit(solution)/shard_map/psum | solution.py:77
  212.7 2.8 fusion.56
  215.6 6.4 %fusion.27 = f32[128,576]{0,1:T(8,128)S(1)} fusion(bf16[2,7168,576]{1,2,0:T(8,128)(2,1)} %param.24, bf16[128,7168]{1,0:T(8,128)(2,1)S(1)} %get-tuple-element.13, f32[7168]{0:T(1024)} %bitcast.194, f32[128]{0:T(128)S(1)} %add_rsqrt_fusion.3), kind=kOutput, calls=%fused_computation.31 | convolution fusion | flops 1060634624 | bytes 10416640 | tf_op jit(solution)/shard_map/dot_general | solution.py:54
  222.3 0.8 fusion.223
  223.1 0.8 multiply_convert_fusion.4
  223.9 10.7 %multiply_reduce_fusion = (f32[128]{0:T(128)}, f32[128,1536]{1,0:T(8,128)}) fusion(bf16[2,7168,1536]{2,1,0:T(8,128)(2,1)} %param.22, bf16[128,7168]{1,0:T(8,128)(2,1)S(1)} %get-tuple-element.13, f32[7168]{0:T(1024)S(1)} %bitcast.195, f32[128]{0:T(128)S(1)} %add_rsqrt_fusion.3), kind=kOutput, calls=%fused_computation.115 | convolution fusion | flops 2822635520 | bytes 24671232 | tf_op jit(solution)/shard_map/dot_general | solution.py:49
  234.6 0.6 maximum_bitcast_fusion.1
  235.2 1.5 copy.41
  236.7 1.8 copy.39
  238.4 1.7 copy.29
  240.1 0.7 add_rsqrt_fusion.2
  240.8 2.0 fusion.155
  242.8 0.3 fusion.83
  243.2 8.1 %fusion.10 = f32[128,4,128]{2,1,0:T(4,128)S(1)} fusion(bf16[2,128,128,512]{3,2,1,0:T(8,128)(2,1)} %param.19, bf16[128,4,512]{2,0,1:T(8,128)(2,1)S(1)} %fusion.83), kind=kOutput, calls=%fused_computation.10 | convolution fusion | flops 67108864 | bytes 17563648 | tf_op jit(solution)/shard_map/bhc,btc->bht/dot_general | solution.py:29
  251.3 0.7 fusion.148
  252.2 0.3 fusion.210
  252.5 2.4 fusion.204
  254.9 0.4 select_reduce_fusion
  255.4 8.1 %fusion.79 = bf16[128,4,512]{2,1,0:T(4,128)(2,1)S(1)} fusion(bf16[2,128,128,512]{3,2,1,0:T(8,128)(2,1)} %param.19, f32[128,512]{1,0:T(8,128)S(1)} %copy-done.11, f32[128,4]{1,0:T(8,128)S(1)} %convert_element_type.214, bf16[128,4,128]{2,1,0:T(4,128)(2,1)S(1)} %get-tuple-element.11, pred[128,128]{1,0:T(8,128)(4,1)S(1)} %get-tuple-element.41), kind=kOutput, calls=%fused_computation.91 | convolution fusion | flops 67960832 | bytes 17713152 | tf_op jit(solution)/shard_map/bht,btc->bhc/dot_general | solution.py:41
  263.5 5.8 %fusion.21 = bf16[128,7168]{1,0:T(8,128)(2,1)} fusion(bf16[2,4,128,7168]{3,2,1,0:T(8,128)(2,1)} %param.29, bf16[512,4,128]{2,1,0:T(4,128)(2,1)S(1)} %copy-done.10, bf16[128,4,512]{2,1,0:T(4,128)(2,1)S(1)} %fusion.79), kind=kOutput, calls=%fused_computation.23 | convolution fusion | flops 1007616000 | bytes 10223616 | tf_op jit(solution)/shard_map/bhv,hvd->bd/dot_general | solution.py:73
  269.4 0.3 all-reduce.11.cloned.1.call-start
  269.7 55.9 %all-reduce.9.cloned.1.call-done = bf16[128,7168]{1,0:T(8,128)(2,1)} async-done(((bf16[128,7168]{1,0:T(8,128)(2,1)}), bf16[128,7168]{1,0:T(8,128)(2,1)}) %all-reduce.9.cloned.1.call-update) | async-done | bytes 1835024 | tf_op jit(solution)/shard_map/psum | solution.py:74
  325.6 2.2 fusion.60
  327.9 1.2 copy-done.4
  329.1 5.7 %fusion.25 = f32[128,576]{0,1:T(8,128)S(1)} fusion(bf16[2,7168,576]{1,2,0:T(8,128)(2,1)} %param.31, bf16[128,7168]{1,0:T(8,128)(2,1)S(1)} %get-tuple-element.9, f32[7168]{0:T(1024)S(1)} %bitcast.196, f32[128]{0:T(128)S(1)} %add_rsqrt_fusion), kind=kOutput, calls=%fused_computation.29 | convolution fusion | flops 1060634624 | bytes 10416640 | tf_op jit(solution)/shard_map/dot_general | solution.py:63
  334.8 14.2 %convolution_convert_fusion = bf16[128,7168]{1,0:T(8,128)(2,1)} fusion(bf16[2,576,7168]{2,1,0:T(8,128)(2,1)} %param.33, bf16[2,7168,576]{1,2,0:T(8,128)(2,1)} %param.32, bf16[128,7168]{1,0:T(8,128)(2,1)} %copy-done.4, f32[7168]{0:T(1024)S(1)} %bitcast.197, f32[128]{0:T(128)S(1)} %add_rsqrt_fusion, f32[128,576]{0,1:T(8,128)S(1)} %fusion.25), kind=kOutput, calls=%fused_computation.24 | convolution fusion | flops 2118959104 | bytes 20509184 | tf_op jit(solution)/shard_map/dot_general | solution.py:66
  349.4 0.9 copy.30
  350.3 0.6 maximum_maximum_fusion
  350.9 54.4 %all-reduce.11.cloned.1.call-done = bf16[128,7168]{1,0:T(8,128)(2,1)} async-done(((bf16[128,7168]{1,0:T(8,128)(2,1)}), bf16[128,7168]{1,0:T(8,128)(2,1)}) %all-reduce.11.cloned.1.call-update) | async-done | bytes 1835024 | tf_op jit(solution)/shard_map/psum | solution.py:77
  405.3 3.2 fusion.63
  (96 shorter events, 1.9 us)
Async XLA Ops:
  7.2 124.5 %all-reduce.5.cloned.1.call-start = ((), (), s32[]{:S(2)}) async-start(), calls=%async_computation | async-start | bytes 3670016 | tf_op jit(solution)/shard_map/psum | solution.py:74
  7.3 13.6 %copy-start.30 = (f32[32]{0:T(128)}, f32[32]{0:T(128)S(1)}, u32[]{:S(2)}) copy-start(f32[32]{0:T(128)S(1)} %multiply_exponential_fusion) | copy-start | bytes 388
  7.9 13.0 %copy-start.32 = (f32[128]{0:T(128)}, f32[128]{0:T(128)S(1)}, u32[]{:S(2)}) copy-start(f32[128]{0:T(128)S(1)} %convert_element_type.191) | copy-start | bytes 1540
  8.7 46.1 %copy-start.24 = (pred[128,128]{1,0:T(8,128)(4,1)}, pred[128,128]{1,0:T(8,128)(4,1)S(1)}, u32[]{:S(2)}) copy-start(pred[128,128]{1,0:T(8,128)(4,1)S(1)} %get-tuple-element.40) | copy-start | bytes 49156
  12.0 8.1 %copy-start.19 = (f32[1,512]{1,0:T(1,128)}, f32[1,512]{1,0:T(1,128)S(1)}, u32[]{:S(2)}) copy-start(f32[1,512]{1,0:T(1,128)S(1)} %get-tuple-element.37) | copy-start | bytes 6148
  13.5 6.8 %copy-start.23 = (bf16[2,1536]{1,0:T(2,128)(2,1)S(1)}, bf16[2,1536]{1,0:T(2,128)(2,1)}, u32[]{:S(2)}) copy-start(bf16[2,1536]{1,0:T(2,128)(2,1)} %param.23) | copy-start | bytes 18436
  13.5 9.3 %copy-start = (bf16[128,7168]{1,0:T(8,128)(2,1)S(1)}, bf16[128,7168]{1,0:T(8,128)(2,1)}, u32[]{:S(2)}) copy-start(bf16[128,7168]{1,0:T(8,128)(2,1)} %param.17) | copy-start | bytes 5505028
  20.0 12.5 %copy-start.26 = (f32[128]{0:T(128)}, f32[128]{0:T(128)S(1)}, u32[]{:S(2)}) copy-start(f32[128]{0:T(128)S(1)} %add_rsqrt_fusion.5) | copy-start | bytes 1540
  22.8 9.7 %copy-start.7 = (bf16[2,512,4,128]{3,2,1,0:T(4,128)(2,1)S(1)}, bf16[2,512,4,128]{3,2,1,0:T(4,128)(2,1)}, u32[]{:S(2)}) copy-start(bf16[2,512,4,128]{3,2,1,0:T(4,128)(2,1)} %param.27) | copy-start | bytes 3145732
  22.8 10.0 %copy-start.8 = (bf16[2,512,4,128]{3,2,1,0:T(4,128)(2,1)S(1)}, bf16[2,512,4,128]{3,2,1,0:T(4,128)(2,1)}, u32[]{:S(2)}) copy-start(bf16[2,512,4,128]{3,2,1,0:T(4,128)(2,1)} %param.28) | copy-start | bytes 3145732
  37.9 0.8 copy-start.6
  38.7 0.8 copy-start.9
  40.8 13.4 %copy-start.15 = (f32[128,1,4]{2,1,0:T(1,128)S(1)}, f32[128,1,4]{2,1,0:T(1,128)}, u32[]{:S(2)}) copy-start(f32[128,1,4]{2,1,0:T(1,128)} %fusion.151) | copy-start | bytes 6148
  53.0 1.8 copy-start.13
  67.9 6.3 %copy-start.14 = (bf16[2,7168]{1,0:T(2,128)(2,1)S(1)}, bf16[2,7168]{1,0:T(2,128)(2,1)}, u32[]{:S(2)}) copy-start(bf16[2,7168]{1,0:T(2,128)(2,1)} %param.30) | copy-start | bytes 86020
  74.0 138.7 %all-reduce.7.cloned.1.call-start = ((), (), s32[]{:S(2)}) async-start(), calls=%async_computation.1 | async-start | bytes 3670016 | tf_op jit(solution)/shard_map/psum | solution.py:77
  134.5 1.2 copy-start.3
  156.5 169.1 %all-reduce.9.cloned.1.call-start = ((), (), s32[]{:S(2)}) async-start(), calls=%async_computation.2 | async-start | bytes 3670016 | tf_op jit(solution)/shard_map/psum | solution.py:74
  215.5 8.3 %copy-start.1 = (bf16[128,7168]{1,0:T(8,128)(2,1)}, bf16[128,7168]{1,0:T(8,128)(2,1)S(1)}, u32[]{:S(2)}) copy-start(bf16[128,7168]{1,0:T(8,128)(2,1)S(1)} %get-tuple-element.13) | copy-start | bytes 5505028
  215.5 6.6 %copy-start.31 = (f32[32]{0:T(128)S(1)}, f32[32]{0:T(128)}, u32[]{:S(2)}) copy-start(f32[32]{0:T(128)} %copy-done.30) | copy-start | bytes 388
  215.5 6.5 %copy-start.33 = (f32[128]{0:T(128)S(1)}, f32[128]{0:T(128)}, u32[]{:S(2)}) copy-start(f32[128]{0:T(128)} %copy-done.32) | copy-start | bytes 1540
  215.6 6.7 %copy-start.17 = (f32[1,512]{1,0:T(1,128)S(1)}, f32[1,512]{1,0:T(1,128)}, u32[]{:S(2)}) copy-start(f32[1,512]{1,0:T(1,128)} %get-tuple-element.36) | copy-start | bytes 6148
  215.6 8.3 %copy-start.21 = (f32[1,7168]{1,0:T(1,128)S(1)}, f32[1,7168]{1,0:T(1,128)}, u32[]{:S(2)}) copy-start(f32[1,7168]{1,0:T(1,128)} %get-tuple-element.34) | copy-start | bytes 86020
  222.3 0.8 copy-start.28
  243.2 8.1 %copy-start.12 = (bf16[128,512,1]{1,2,0:T(2,128)(2,1)S(1)}, bf16[128,512,1]{1,2,0:T(2,128)(2,1)}, u32[]{:S(2)}) copy-start(bf16[128,512,1]{1,2,0:T(2,128)(2,1)} %copy.39) | copy-start | bytes 393220
  243.2 9.0 %copy-start.16 = (bf16[128,64,1]{1,2,0:T(2,128)(2,1)S(1)}, bf16[128,64,1]{1,2,0:T(2,128)(2,1)}, u32[]{:S(2)}) copy-start(bf16[128,64,1]{1,2,0:T(2,128)(2,1)} %copy.41) | copy-start | bytes 49156
  243.2 9.3 %copy-start.25 = (pred[128,128]{1,0:T(8,128)(4,1)S(1)}, pred[128,128]{1,0:T(8,128)(4,1)}, u32[]{:S(2)}) copy-start(pred[128,128]{1,0:T(8,128)(4,1)} %copy-done.24) | copy-start | bytes 49156
  251.3 4.0 copy-start.11
  255.4 8.1 %copy-start.10 = (bf16[512,4,128]{2,1,0:T(4,128)(2,1)S(1)}, bf16[512,4,128]{2,1,0:T(4,128)(2,1)}, u32[]{:S(2)}) copy-start(bf16[512,4,128]{2,1,0:T(4,128)(2,1)} %get-tuple-element.23) | copy-start | bytes 1572868
  263.5 62.1 %copy-start.2 = (bf16[128,7168]{1,0:T(8,128)(2,1)S(1)}, bf16[128,7168]{1,0:T(8,128)(2,1)}, u32[]{:S(2)}) copy-start(bf16[128,7168]{1,0:T(8,128)(2,1)} %copy-done.1) | copy-start | bytes 5505028
  269.3 59.8 %copy-start.22 = (f32[1,7168]{1,0:T(1,128)S(1)}, f32[1,7168]{1,0:T(1,128)}, u32[]{:S(2)}) copy-start(f32[1,7168]{1,0:T(1,128)} %get-tuple-element.32) | copy-start | bytes 86020
  269.4 135.9 %all-reduce.11.cloned.1.call-start = ((), (), s32[]{:S(2)}) async-start(), calls=%async_computation.3 | async-start | bytes 3670016 | tf_op jit(solution)/shard_map/psum | solution.py:77
  327.8 1.2 copy-start.4
  334.8 14.3 %copy-start.20 = (f32[1,512]{1,0:T(1,128)S(1)}, f32[1,512]{1,0:T(1,128)}, u32[]{:S(2)}) copy-start(f32[1,512]{1,0:T(1,128)} %copy-done.19) | copy-start | bytes 6148
  334.8 14.3 %copy-start.27 = (f32[128]{0:T(128)S(1)}, f32[128]{0:T(128)}, u32[]{:S(2)}) copy-start(f32[128]{0:T(128)} %copy-done.26) | copy-start | bytes 1540
  334.8 14.4 %copy-start.18 = (f32[1,512]{1,0:T(1,128)S(1)}, f32[1,512]{1,0:T(1,128)}, u32[]{:S(2)}) copy-start(f32[1,512]{1,0:T(1,128)} %get-tuple-element.36) | copy-start | bytes 6148
  334.8 14.4 %copy-start.29 = (f32[128]{0:T(128)S(1)}, f32[128]{0:T(128)}, u32[]{:S(2)}) copy-start(f32[128]{0:T(128)} %copy-done.28) | copy-start | bytes 1540
  349.0 56.3 %copy-start.5 = (bf16[128,7168]{1,0:T(8,128)(2,1)S(1)}, bf16[128,7168]{1,0:T(8,128)(2,1)}, u32[]{:S(2)}) copy-start(bf16[128,7168]{1,0:T(8,128)(2,1)} %copy-done.4) | copy-start | bytes 5505028
Sparse Core Ops, SparseCore 0:
  74.2 57.5 all-reduce.4
  156.6 56.0 all-reduce.6
  269.5 56.0 all-reduce.8
  349.2 56.0 all-reduce.10
where the time goes:
time: 421 us; the launch traced here: 415 us
  waiting for transfers between devices  223 us (53%)
  matrix products  134 us (32%)
  other arithmetic  26.1 us (6%)
  local copies, waits for them, and re-layouts  16.1 us (4%)
  between operations  14.7 us (3%)
    psum x2, waiting for transfers between devices, local_layer(): attn_sum = lax.psum(attn_part, 'tp')  113 us
    psum x2, waiting for transfers between devices, local_layer(): mlp_sum = lax.psum(mlp_part, 'tp')  110 us
    dot_general x2, matrix products, gated_mlp(): return jnp.dot(act_out, w_down, preferred_element_type=jnp.float32)  28.4 us
    dot_general x2, matrix products, attention_heads(): jnp.dot(normed, w_dq, preferred_element_type=jnp.float32)  20.4 us
    dot_general x2, matrix products, latent_attention(): jnp.einsum('bhc,btc->bht', q_lat, ckv_old, preferred_element_type=jnp.flo...  19.2 us
    dot_general x2, matrix products, latent_attention(): jnp.einsum('bht,btc->bhc', jnp.where(at_pos, bf_zero, attn_prob), ckv_old...  17 us
    dot_general x2, matrix products, attention_heads(): kv_lat = jnp.dot(normed, w_dkv, preferred_element_type=jnp.float32)  12.8 us
    dot_general x2, matrix products, gated_mlp(): gate_pre = jnp.dot(mlp_in, w_gate, preferred_element_type=jnp.float32)  12.1 us
  transfers between devices with their start and end apart: 4, of which 4 were waited for; matrix products, arithmetic and copies ran while one was open for 1% of the time, Pallas kernels for 0%

commit v1 on v0

v1 whole, which is shorter than its diff:
```python
import math
import functools
import jax
import jax.numpy as jnp
from jax import lax
from jax.experimental import pallas as pl
from jax.experimental.pallas import tpu as pltpu
from jax.sharding import PartitionSpec as P

NORM_EPS = 1e-6
ROPE_BASE = 10000.0
F32 = jnp.float32
BF16 = jnp.bfloat16
MESH = pl.DeviceIdType.MESH
NEG_INF = float('-inf')


def rms(values, gain):
    inv = lax.rsqrt(jnp.mean(values * values, axis=-1, keepdims=True) + NORM_EPS)
    return values * inv * gain


def dot_nt(lhs, rhs):
    return lax.dot_general(lhs, rhs, (((1,), (1,)), ((), ())), preferred_element_type=F32)


def dot_nn(lhs, rhs):
    return jnp.dot(lhs, rhs, preferred_element_type=F32)


def swap_halves(values, half):
    width = values.shape[-1]
    lane = lax.broadcasted_iota(jnp.int32, values.shape, 1)
    up = pltpu.roll(values, half, 1)
    down = pltpu.roll(values, width - half, 1)
    return jnp.where(lane % (2 * half) < half, down, up)


def tile_rows(values, count):
    return jnp.concatenate([values] * count, axis=0)


def step_kernel(cfg, x_hbm, cos_ref, sin_ref, pos_ref, ag_ref, mg_ref, qg_ref, kg_ref,
                wdq, wkv, wuq, wuk, wuv, wo, wg, wu, wd, ckv_hbm, kpe_hbm,
                x_out, ckv_out, kpe_out,
                xb, a_buf, b_all, q_all, acc_q, acc_kv, u_buf, r_buf, ctx_buf, o_buf, wf,
                gate_acc, up_acc, act_buf,
                part, d2d, psum, rel, cmb, fin,
                dq_buf, kv_buf, uq_buf, uk_buf, uv_buf, wo_buf, wg_buf, wu_buf, wd_buf, ckv_buf, kpe_buf,
                x_sem, dq_sem, kv_sem, w_sem, c_sem, out_sem,
                ag_send, ag_recv, rs_send, rs_recv):
    tp_size, layers, heads, kc, slots, chunks, seqs = (
        cfg['tp'], cfg['layers'], cfg['heads'], cfg['kc'], cfg['slots'], cfg['chunks'], cfg['seqs'])
    nchip = tp_size // 2
    model = xb.shape[1]
    rows = xb.shape[0]
    lora = uq_buf.shape[1]
    latent = ckv_buf.shape[-1]
    rope = kpe_buf.shape[2]
    nope = uk_buf.shape[1]
    keys = ckv_buf.shape[2]
    batch = rows * tp_size
    n_dq = model // kc
    cw = model // chunks
    ch = cw // 2
    scale = float((nope + rope) ** -0.5)

    me = lax.axis_index('tp')
    core = lax.rem(me, 2)
    chip = me // 2
    other = 1 - core
    rchip = lax.rem(chip + 1, nchip)
    lchip = lax.rem(chip + nchip - 1, nchip)
    ochip = lax.rem(chip + 2, nchip)
    mate = 2 * chip + other
    right = 2 * rchip + core
    left = 2 * lchip + core
    opp = 2 * ochip + core

    barrier = pltpu.get_barrier_semaphore()
    for peer in (mate, right, left):
        pl.semaphore_signal(barrier, inc=1, device_id={'tp': peer}, device_id_type=MESH)

    def x_copy():
        return pltpu.make_async_copy(x_hbm.at[me], xb, x_sem)

    def dq_copy(layer, i, slot):
        off = pl.multiple_of(i * kc, 128)
        return pltpu.make_async_copy(wdq.at[layer, pl.ds(off, kc), :], dq_buf.at[slot], dq_sem.at[slot])

    def kv_copy(layer, i, slot):
        off = pl.multiple_of(i * kc, 128)
        return pltpu.make_async_copy(wkv.at[layer, :, pl.ds(off, kc)], kv_buf.at[slot], kv_sem.at[slot])

    weights = [(wuq, uq_buf), (wuk, uk_buf), (wuv, uv_buf), (wo, wo_buf), (wg, wg_buf), (wu, wu_buf), (wd, wd_buf)]

    def w_copy(layer, idx):
        src, dst = weights[idx]
        return pltpu.make_async_copy(src.at[layer], dst, w_sem.at[idx])

    def ckv_copy(layer, g, slot):
        return pltpu.make_async_copy(ckv_hbm.at[layer, pl.ds(g * seqs, seqs)], ckv_buf.at[slot], c_sem.at[0, slot])

    def kpe_copy(layer, g, slot):
        return pltpu.make_async_copy(kpe_hbm.at[layer, pl.ds(g * seqs, seqs)], kpe_buf.at[slot], c_sem.at[1, slot])

    def start_dq(layer):
        for s in range(slots):
            dq_copy(layer, s, s).start()
            kv_copy(layer, s, s).start()

    def start_cache(layer):
        for s in range(2):
            ckv_copy(layer, s, s).start()
            kpe_copy(layer, s, s).start()

    def remote(src, dst, sems, recvs, j, kind, dev):
        return pltpu.make_async_remote_copy(src_ref=src, dst_ref=dst, send_sem=sems.at[j, kind],
                                            recv_sem=recvs.at[j, kind], device_id={'tp': dev}, device_id_type=MESH)

    def ag_desc(buf, j, spec, kind, blk, dev):
        off, half_a, width = spec
        lo, size = off, width
        if kind in (3, 7):
            size = half_a
        elif kind in (4, 8):
            lo, size = off + half_a, width - half_a
        ref = buf.at[blk, :, pl.ds(lo, size)]
        return remote(ref, ref, ag_send, ag_recv, j, kind, dev)

    mleft = 2 * lchip + other
    mright = 2 * rchip + other
    mopp = 2 * ochip + other
    ag_out = [(me, mate), (me, right), (me, left), (left, right), (right, left), (left, mate), (right, mate), (opp, mate), (opp, mate)]
    ag_in = [mate, left, right, opp, opp, mleft, mright, mopp, mopp]

    def ag_start(buf, j, spec, kind):
        ag_desc(buf, j, spec, kind, *ag_out[kind]).start()

    def ag_wait(buf, j, spec, kind):
        ag_desc(buf, j, spec, kind, ag_in[kind], mate).wait_recv()

    def all_gather(buf, specs, consume):
        n = len(specs)
        for j in range(n):
            for kind in (1, 2, 0):
                ag_start(buf, j, specs[j], kind)

        def forward(j):
            ag_wait(buf, j, specs[j], 1)
            ag_start(buf, j, specs[j], 3)
            ag_start(buf, j, specs[j], 5)
            ag_wait(buf, j, specs[j], 2)
            ag_start(buf, j, specs[j], 4)
            ag_start(buf, j, specs[j], 6)

        def finish(j):
            ag_wait(buf, j, specs[j], 3)
            ag_start(buf, j, specs[j], 7)
            ag_wait(buf, j, specs[j], 4)
            ag_start(buf, j, specs[j], 8)
            for kind in (0, 5, 6, 7, 8):
                ag_wait(buf, j, specs[j], kind)
            consume(j)

        forward(0)
        for j in range(1, n):
            forward(j)
            finish(j - 1)
        finish(n - 1)
        for j in range(n):
            for kind in range(9):
                ag_desc(buf, j, specs[j], kind, *ag_out[kind]).wait_send()

    def rs_desc(j, kind):
        o = j * cw
        ca, cb = pl.ds(o, ch), pl.ds(o + ch, ch)
        hj = pl.ds(j * ch, ch)
        full = pl.ds(o, cw)
        src, dst, dev = [
            lambda: (part.at[:, other, :, full], d2d.at[:, :, full], mate),
            lambda: (psum.at[ochip, :, ca], rel.at[0, :, hj], right),
            lambda: (psum.at[ochip, :, cb], rel.at[1, :, hj], left),
            lambda: (psum.at[rchip, :, cb], fin.at[0, :, cb], right),
            lambda: (psum.at[lchip, :, ca], fin.at[1, :, ca], left),
            lambda: (cmb.at[0, :, hj], fin.at[0, :, ca], right),
            lambda: (cmb.at[1, :, hj], fin.at[1, :, cb], left),
        ][kind]()
        return remote(src, dst, rs_send, rs_recv, j, kind, dev)

    def reduce_scatter(product):
        def mm(j):
            val = product(j)
            part[:, :, :, pl.ds(j * cw, cw)] = val.reshape(nchip, 2, rows, cw).astype(BF16)
            rs_desc(j, 0).start()

        def pair(j):
            rs_desc(j, 0).wait_recv()
            cols = pl.ds(j * cw, cw)
            for cc in range(nchip):
                psum[cc, :, cols] = (part[cc, core, :, cols].astype(F32) + d2d[cc, :, cols].astype(F32)).astype(BF16)
            for kind in (1, 2, 3, 4):
                rs_desc(j, kind).start()

        def combine(j):
            o = j * cw
            hj = pl.ds(j * ch, ch)
            rs_desc(j, 1).wait_recv()
            cmb[0, :, hj] = (psum[rchip, :, pl.ds(o, ch)].astype(F32) + rel[0, :, hj].astype(F32)).astype(BF16)
            rs_desc(j, 5).start()
            rs_desc(j, 2).wait_recv()
            cmb[1, :, hj] = (psum[lchip, :, pl.ds(o + ch, ch)].astype(F32) + rel[1, :, hj].astype(F32)).astype(BF16)
            rs_desc(j, 6).start()

        def final(j):
            for kind in (3, 4, 5, 6):
                rs_desc(j, kind).wait_recv()
            cols = pl.ds(j * cw, cw)
            total = psum[chip, :, cols].astype(F32) + fin[0, :, cols].astype(F32) + fin[1, :, cols].astype(F32)
            xb[:, cols] = (xb[:, cols].astype(F32) + total).astype(BF16)

        for j in range(chunks + 2):
            if j < chunks:
                mm(j)
            if 0 <= j - 1 < chunks:
                pair(j - 1)
            if 0 <= j - 2 < chunks:
                combine(j - 2)
        return final

    def rs_drain(final):
        for j in range(chunks):
            final(j)
        for j in range(chunks):
            for kind in range(7):
                rs_desc(j, kind).wait_send()

    b_specs = [(j * cw, ch, cw) for j in range(chunks)]
    qw = q_all.shape[2]
    q_specs = [(0, (qw // 256 + 1) * 128 if (qw // 128) % 2 else qw // 2, qw)]

    def gain_row(ref, layer):
        vals = ref[...].astype(F32)
        row = vals[0:1]
        for i in range(1, layers):
            row = jnp.where(layer == i, vals[i:i + 1], row)
        return row

    x_copy().start()
    start_dq(0)
    pl.semaphore_wait(barrier, 3)
    x_copy().wait()

    def layer_body(layer, carry):
        more = layer + 1 < layers
        a_buf[...] = rms(xb[...].astype(F32), gain_row(ag_ref, layer)).astype(BF16)
        acc_q[...] = jnp.zeros_like(acc_q)
        acc_kv[...] = jnp.zeros_like(acc_kv)

        def dq_step(i, c):
            slot = lax.rem(i, slots)
            dq_copy(layer, i, slot).wait()
            kv_copy(layer, i, slot).wait()
            a_c = a_buf[:, pl.ds(pl.multiple_of(i * kc, 128), kc)]
            acc_q[...] += dot_nn(a_c, dq_buf[slot])
            acc_kv[...] += dot_nt(kv_buf[slot], a_c)

            @pl.when(i + slots < n_dq)
            def _():
                dq_copy(layer, i + slots, slot).start()
                kv_copy(layer, i + slots, slot).start()
            return c

        lax.fori_loop(0, n_dq, dq_step, 0)

        @pl.when(layer == 0)
        def _():
            for idx in (0, 1, 2):
                w_copy(layer, idx).start()
            start_cache(layer)
            for idx in (3, 4, 5, 6):
                w_copy(layer, idx).start()

        q_all[me, :, pl.ds(0, lora)] = rms(acc_q[...], gain_row(qg_ref, layer)).astype(BF16)
        kv = jnp.transpose(acc_kv[...])
        q_all[me, :, pl.ds(lora, latent)] = rms(kv[:, :latent], gain_row(kg_ref, layer)).astype(BF16)
        row0 = pl.multiple_of(me * rows, rows)
        kr = kv[:, latent:latent + rope]
        kr = jnp.concatenate([kr, kr], axis=1)
        kr = kr * cos_ref[pl.ds(row0, rows), 0:2 * rope] + swap_halves(kr, rope // 2) * sin_ref[pl.ds(row0, rows), 0:2 * rope]
        lane = lax.broadcasted_iota(jnp.int32, kr.shape, 1)
        q_all[me, :, pl.ds(lora + latent, 2 * rope)] = jnp.where(lane < rope, kr, 0.0).astype(BF16)

        def nothing(j):
            return None

        all_gather(q_all, q_specs, nothing)

        out_c = pltpu.make_async_copy(q_all.at[:, :, pl.ds(lora, latent)], ckv_out.at[layer], out_sem.at[0])
        out_k = pltpu.make_async_copy(q_all.at[:, :, pl.ds(lora + latent, 2 * rope)], kpe_out.at[layer], out_sem.at[1])
        out_c.start()
        out_k.start()

        w_copy(layer, 0).wait()
        c_q = q_all[:, :, pl.ds(0, lora)].reshape(batch, lora)
        per = nope + rope
        w_n = jnp.concatenate([uq_buf[pl.ds(h * per, nope), :] for h in range(heads)], axis=0)
        w_r = jnp.concatenate([uq_buf[pl.ds(h * per + nope, rope), :] for h in range(heads)], axis=0)
        q_n = dot_nt(c_q, w_n).astype(BF16)
        q_r = dot_nt(c_q, w_r)
        q_r = q_r * cos_ref[...] + swap_halves(q_r, rope // 2) * sin_ref[...]
        lane2 = lax.broadcasted_iota(jnp.int32, (batch, 2 * rope), 1)
        for pair_i in range(heads // 2):
            duo = q_r[:, pair_i * 2 * rope:(pair_i + 1) * 2 * rope]
            swp = pltpu.roll(duo, rope, 1)
            r_buf[2 * pair_i] = jnp.where(lane2 < rope, duo, swp).astype(BF16)
            r_buf[2 * pair_i + 1] = jnp.where(lane2 < rope, swp, duo).astype(BF16)
        w_copy(layer, 1).wait()
        wf[...] = uk_buf[...].astype(F32)
        for h in range(heads):
            wk_h = wf[pl.ds(h, latent, stride=heads), :].astype(BF16)
            u_buf[h] = dot_nt(q_n[:, h * nope:(h + 1) * nope], wk_h).astype(BF16)

        @pl.when(more)
        def _():
            w_copy(layer + 1, 0).start()
            w_copy(layer + 1, 1).start()

        m_rows = heads * seqs

        def att_step(g, c):
            slot = lax.rem(g, 2)
            ckv_copy(layer, g, slot).wait()
            kpe_copy(layer, g, slot).wait()
            r0 = pl.multiple_of(g * seqs, seqs)
            cache = ckv_buf[slot].reshape(seqs * keys, latent)
            u_g = u_buf[:, pl.ds(r0, seqs), :].reshape(m_rows, latent)
            r_g = r_buf[:, pl.ds(r0, seqs), :].reshape(m_rows, 2 * rope).astype(F32)
            u_2 = jnp.concatenate([u_g, u_g], axis=0)
            s_t = dot_nt(cache, u_2)
            lane_t = lax.broadcasted_iota(jnp.int32, (keys, 2 * m_rows), 1) % seqs
            sel = s_t[0:keys]
            for b in range(1, seqs):
                sel = jnp.where(lane_t == b, s_t[b * keys:(b + 1) * keys], sel)
            s_n = jnp.transpose(sel)[0:m_rows]
            row_b = lax.broadcasted_iota(jnp.int32, (m_rows, keys), 0) % seqs
            lane_k = lax.broadcasted_iota(jnp.int32, (m_rows, keys), 1)
            row_r = lax.broadcasted_iota(jnp.int32, (m_rows, 2 * rope), 0) % seqs
            lane_r = lax.broadcasted_iota(jnp.int32, (m_rows, 2 * rope), 1) // rope
            q_blk = jnp.concatenate(
                [jnp.where(row_r == 2 * b + lane_r, r_g, 0.0).astype(BF16) for b in range(seqs // 2)], axis=1)
            s_r = dot_nn(q_blk, kpe_buf[slot].reshape(seqs * rope, keys))
            cn = tile_rows(q_all[g, :, pl.ds(lora, latent)].astype(F32), heads)
            kn = tile_rows(q_all[g, :, pl.ds(lora + latent, 2 * rope)].astype(F32), heads)
            fresh = jnp.sum(u_g.astype(F32) * cn, axis=-1, keepdims=True) + jnp.sum(r_g * kn, axis=-1, keepdims=True)
            pos = tile_rows(pos_ref[pl.ds(r0, seqs), :], heads)
            at_pos = lane_k == pos
            s = jnp.where(at_pos, fresh, s_n + s_r) * scale
            s = jnp.where(lane_k <= pos, s, NEG_INF)
            e = jnp.exp(s - jnp.max(s, axis=-1, keepdims=True))
            prob = (e / jnp.sum(e, axis=-1, keepdims=True)).astype(BF16).astype(F32)
            p_new = jnp.sum(jnp.where(at_pos, prob, 0.0), axis=-1, keepdims=True)
            p_old = jnp.where(at_pos, 0.0, prob)
            p_blk = jnp.concatenate([jnp.where(row_b == b, p_old, 0.0).astype(BF16) for b in range(seqs)], axis=1)
            ctx = dot_nn(p_blk, cache) + p_new * cn
            ctx_buf[:, pl.ds(r0, seqs), :] = ctx.astype(BF16).reshape(heads, seqs, latent)

            @pl.when(g + 2 < batch // seqs)
            def _():
                ckv_copy(layer, g + 2, slot).start()
                kpe_copy(layer, g + 2, slot).start()
            return c

        lax.fori_loop(0, batch // seqs, att_step, 0)

        w_copy(layer, 2).wait()
        wf[...] = uv_buf[...].astype(F32)
        for h in range(heads):
            wv_h = wf[pl.ds(h, latent, stride=heads), :].astype(BF16)
            o_buf[:, h * nope:(h + 1) * nope] = dot_nn(ctx_buf[h], wv_h).astype(BF16)

        @pl.when(more)
        def _():
            w_copy(layer + 1, 2).start()

        w_copy(layer, 3).wait()
        out_c.wait()
        out_k.wait()

        final = reduce_scatter(lambda j: dot_nn(o_buf[...], wo_buf[:, pl.ds(j * cw, cw)]))

        @pl.when(more)
        def _():
            start_dq(layer + 1)
            start_cache(layer + 1)
            w_copy(layer + 1, 3).start()

        rs_drain(final)

        b_all[me] = rms(xb[...].astype(F32), gain_row(mg_ref, layer)).astype(BF16)
        w_copy(layer, 4).wait()
        w_copy(layer, 5).wait()

        def gate_up(j):
            cols = pl.ds(j * cw, cw)
            b_c = b_all[:, :, cols].reshape(batch, cw)
            g_v = dot_nt(wg_buf[:, cols], b_c)
            u_v = dot_nt(wu_buf[:, cols], b_c)
            if j == 0:
                gate_acc[...] = g_v
                up_acc[...] = u_v
            else:
                gate_acc[...] += g_v
                up_acc[...] += u_v

        all_gather(b_all, b_specs, gate_up)
        gate = gate_acc[...]
        act_buf[...] = jnp.transpose(gate * lax.logistic(gate) * up_acc[...]).astype(BF16)
        w_copy(layer, 6).wait()

        @pl.when(more)
        def _():
            w_copy(layer + 1, 4).start()
            w_copy(layer + 1, 5).start()

        final2 = reduce_scatter(lambda j: dot_nn(act_buf[...], wd_buf[:, pl.ds(j * cw, cw)]))

        @pl.when(more)
        def _():
            w_copy(layer + 1, 6).start()

        rs_drain(final2)
        return carry

    lax.fori_loop(0, layers, layer_body, 0)

    b_all[me] = xb[...]

    def put(j):
        cols = pl.ds(j * cw, cw)
        pltpu.make_async_copy(b_all.at[:, :, cols], x_out.at[:, :, cols], out_sem.at[j]).start()

    all_gather(b_all, b_specs, put)
    for j in range(chunks):
        cols = pl.ds(j * cw, cw)
        pltpu.make_async_copy(b_all.at[:, :, cols], x_out.at[:, :, cols], out_sem.at[j]).wait()


def solution(mesh):
    tp = mesh.shape['tp']
    cache_spec = P(None, 'dp', None, None)
    head_spec = P(None, None, 'tp', None)
    weight_specs = (P(), P(), P(), P(), P(), head_spec, head_spec, head_spec, P(None, 'tp', None, None), P(), P(None, None, 'tp'), P(None, None, 'tp'), P(None, 'tp', None))
    in_specs = (P('dp', None), P('dp'), cache_spec, cache_spec) + weight_specs
    out_specs = (P('dp', None), P(None, 'dp', None), P(None, 'dp', None))

    def device_body(x_in, pos_ids, ckv_cache, kpe_cache, attn_gain, w_dq, q_gain, w_dkv, kv_gain, w_uq, w_uk, w_uv, w_o,
                    mlp_gain, w_gate, w_up, w_down):
        batch, model = x_in.shape
        layers, _, keys, latent = ckv_cache.shape
        rope = kpe_cache.shape[-1]
        lora = w_dq.shape[-1]
        heads, per = w_uq.shape[2:]
        nope = w_uk.shape[-1]
        ffn = w_gate.shape[-1]
        rows = batch // tp
        kc, slots, chunks, seqs = 512, 4, 4, rows
        half = rope // 2

        inv_freq = jnp.exp(jnp.arange(half, dtype=F32) * (-2.0 * math.log(ROPE_BASE) / rope))
        angles = pos_ids.astype(F32)[:, None] * inv_freq
        cos, sin = jnp.cos(angles), jnp.sin(angles)
        cos_t = jnp.tile(jnp.concatenate([cos, cos], axis=1), (1, heads))
        sin_t = jnp.tile(jnp.concatenate([-sin, sin], axis=1), (1, heads))
        pos_t = jnp.broadcast_to(pos_ids[:, None], (batch, keys))

        vm = pl.BlockSpec(memory_space=pltpu.VMEM)
        hb = pl.BlockSpec(memory_space=pl.ANY)
        dma = pltpu.SemaphoreType.DMA
        qw = lora + latent + 2 * rope
        ch = model // chunks // 2
        scratch = [
            pltpu.VMEM((rows, model), BF16),
            pltpu.VMEM((rows, model), BF16),
            pltpu.VMEM((tp, rows, model), BF16),
            pltpu.VMEM((tp, rows, qw), BF16),
            pltpu.VMEM((rows, lora), F32),
            pltpu.VMEM((latent + rope, rows), F32),
            pltpu.VMEM((heads, batch, latent), BF16),
            pltpu.VMEM((heads, batch, 2 * rope), BF16),
            pltpu.VMEM((heads, batch, latent), BF16),
            pltpu.VMEM((batch, heads * nope), BF16),
            pltpu.VMEM((latent * heads, nope), F32),
            pltpu.VMEM((ffn, batch), F32),
            pltpu.VMEM((ffn, batch), F32),
            pltpu.VMEM((batch, ffn), BF16),
            pltpu.VMEM((tp // 2, 2, rows, model), BF16),
            pltpu.VMEM((tp // 2, rows, model), BF16),
            pltpu.VMEM((tp // 2, rows, model), BF16),
            pltpu.VMEM((2, rows, model // 2), BF16),
            pltpu.VMEM((2, rows, model // 2), BF16),
            pltpu.VMEM((2, rows, model), BF16),
            pltpu.VMEM((slots, kc, lora), BF16),
            pltpu.VMEM((slots, latent + rope, kc), BF16),
            pltpu.VMEM((heads * per, lora), BF16),
            pltpu.VMEM((latent * heads, nope), BF16),
            pltpu.VMEM((latent * heads, nope), BF16),
            pltpu.VMEM((heads * nope, model), BF16),
            pltpu.VMEM((ffn, model), BF16),
            pltpu.VMEM((ffn, model), BF16),
            pltpu.VMEM((ffn, model), BF16),
            pltpu.VMEM((2, seqs, keys, latent), BF16),
            pltpu.VMEM((2, seqs, rope, keys), BF16),
            dma(()), dma((slots,)), dma((slots,)), dma((7,)), dma((2, 2)), dma((max(chunks, 2),)),
            dma((chunks, 9)), dma((chunks, 9)), dma((chunks, 7)), dma((chunks, 7)),
        ]
        cfg = dict(tp=tp, layers=layers, heads=heads, kc=kc, slots=slots, chunks=chunks, seqs=seqs)
        call = pl.pallas_call(
            functools.partial(step_kernel, cfg),
            out_shape=(jax.ShapeDtypeStruct((tp, rows, model), BF16),
                       jax.ShapeDtypeStruct((layers, tp, rows, latent), BF16),
                       jax.ShapeDtypeStruct((layers, tp, rows, 2 * rope), BF16)),
            in_specs=[hb, vm, vm, vm, vm, vm, vm, vm] + [hb] * 11,
            out_specs=(hb, hb, hb),
            scratch_shapes=scratch,
            compiler_params=pltpu.CompilerParams(collective_id=0, has_side_effects=True, vmem_limit_bytes=67043328),
            name='decode_step',
        )
        x_o, c_o, k_o = call(
            x_in.reshape(tp, rows, model), cos_t, sin_t, pos_t, attn_gain, mlp_gain, q_gain, kv_gain,
            w_dq, w_dkv.transpose(0, 2, 1), w_uq.transpose(0, 2, 3, 1).reshape(layers, heads * per, lora),
            w_uk.reshape(layers, latent * heads, nope), w_uv.reshape(layers, latent * heads, nope),
            w_o.reshape(layers, heads * nope, model),
            w_gate.transpose(0, 2, 1), w_up.transpose(0, 2, 1), w_down,
            ckv_cache, kpe_cache.transpose(0, 1, 3, 2))
        return (x_o.reshape(batch, model), c_o.reshape(layers, batch, latent),
                k_o.reshape(layers, batch, 2 * rope)[..., :rope])

    return jax.shard_map(device_body, mesh=mesh, in_specs=in_specs, out_specs=out_specs, check_vma=False)
```

time: 421 us -> 197 us (0.47); the launches traced: 415 us -> 197 us
  waiting for transfers between devices: 223 us -> 0 us
  Pallas kernels: 0 us -> 186 us
  matrix products: 134 us -> 0 us
  other arithmetic: 26.1 us -> 0.82 us
  between operations: 14.7 us -> 0.66 us
  local copies, waits for them, and re-layouts: 16.1 us -> 8.96 us
    psum x4 -> x0, waiting for transfers between devices: 223 us -> none  [the longest x2 113 us: local_layer(): attn_sum = lax.psum(attn_part, 'tp')]
    pallas_call x0 -> x1, Pallas kernels: none -> 186 us  [device_body(): call(x_in.reshape(tp, rows, model), cos_t, sin_t, pos_t, attn_gain, mlp_g...]
    dot_general x20 -> x0, matrix products: 126 us -> none  [the longest x2 28.4 us: gated_mlp(): return jnp.dot(act_out, w_down, preferred_element_type=jnp.float32)]
    reduce_sum x8 -> x0, other arithmetic: 11.5 us -> none  [the longest x6 9.91 us: rms_norm(): jnp.mean(values * values, axis=-1, keepdims=True) + NORM_EPS]
    sub x2 -> x0, matrix products: 5.48 us -> none  [latent_attention(): attn_prob = jax.nn.softmax(scores, axis=-1).astype(jnp.bfloat16)]
    convert_element_type x8 -> x1, other arithmetic: 5.67 us -> 0.66 us  [device_body(): angles = pos_ids.astype(F32)[:, None] * inv_freq]
    convert_element_type x4 -> x0, local copies, waits for them, and re-layouts: 4.49 us -> none  [the longest x2 2.53 us: latent_attention(): ckv_new.astype(jnp.float32)[:, None, :]]
  transfers between devices with their start and end apart: 4 -> 0, of which waited for: 4 -> 0; matrix products, arithmetic and copies ran while one was open for 1% -> 0% of each run, Pallas kernels for 0% -> 0%
where the time goes in v1:
time: 197 us
  Pallas kernels  186 us (94%)
  local copies, waits for them, and re-layouts  8.96 us (5%)
    pallas_call x1, Pallas kernels, device_body(): call(x_in.reshape(tp, rows, model), cos_t, sin_t, pos_t, attn_gain, mlp_g...  186 us
    unnamed x3, local copies, waits for them, and re-layouts  6.06 us

profile of v1, /device:TPU:113, one launch (start us, length us, event | category | flops | bytes accessed | tf_op | source)
XLA Modules:
  0.0 196.6 jit_solution(16843288106965969749)
XLA Ops:
  0.6 0.7 convert_element_type.3
  1.3 0.1 fusion
  1.5 1.4 broadcast_in_dim.2.pos_ref
  2.9 0.8 copy.21.cos_ref
  3.6 0.8 copy.22.sin_ref
  4.4 186.1 %decode_step.1 = (bf16[8,16,7168]{2,1,0:T(8,128)(2,1)}, bf16[2,8,16,512]{3,2,1,0:T(8,128)(2,1)}, bf16[2,8,16,128]{3,2,1,0:T(8,128)(2,1)}) custom-call(bf16[8,16,7168]{2,1,0:T(8,128)(2,1)} %bitcast.23, f32[128,256]{1,0:T(8,128)} %copy.21.cos_ref, f32[128,256]{1,0:T(8,128)} %copy.22.sin_ref, s32[128,128]{1,0:T(8,128)} %broadcast_in_dim.2.pos_ref, ...), custom_call_target="tpu_custom_call" | custom-call | tf_op jit(solution)/shard_map/decode_step/pallas_call | solution.py:529
  190.5 1.5 copy.24
  192.0 2.8 %copy.27 = bf16[128,7168]{1,0:T(8,128)(2,1)} copy(bf16[128,7168]{1,0:T(8,128)(2,1)} %bitcast.24) | data formatting | bytes 3670016
  194.9 1.7 copy.28
  (4 shorter events, 0.0 us)

commit v2 on v1

--- a/solution.py
+++ b/solution.py
@@ -40,14 +40,15 @@
     return jnp.concatenate([values] * count, axis=0)
 
 
-def step_kernel(cfg, x_hbm, cos_ref, sin_ref, pos_ref, ag_ref, mg_ref, qg_ref, kg_ref,
+def step_kernel(cfg, x_hbm, pos_hbm, ag_hbm, mg_hbm, qg_hbm, kg_hbm,
                 wdq, wkv, wuq, wuk, wuv, wo, wg, wu, wd, ckv_hbm, kpe_hbm,
                 x_out, ckv_out, kpe_out,
-                xb, a_buf, b_all, q_all, acc_q, acc_kv, u_buf, r_buf, ctx_buf, o_buf, wf,
-                gate_acc, up_acc, act_buf,
+                pos_row, ag_ref, mg_ref, qg_ref, kg_ref, cos_ref, sin_ref, pos_ref,
+                xb, a_buf, a_pair, acc_in, b_all, q_all, acc_q, u_buf, r_buf, ctx_buf, o_buf, wf,
+                gu_acc, act_buf,
                 part, d2d, psum, rel, cmb, fin,
-                dq_buf, kv_buf, uq_buf, uk_buf, uv_buf, wo_buf, wg_buf, wu_buf, wd_buf, ckv_buf, kpe_buf,
-                x_sem, dq_sem, kv_sem, w_sem, c_sem, out_sem,
+                dq_buf, kv_buf, uq_buf, uk_buf, uv_buf, wo_buf, wgu_buf, wd_buf, ckv_buf, kpe_buf,
+                x_sem, s_sem, px_sem, dq_sem, kv_sem, w_sem, c_sem, out_sem,
                 ag_send, ag_recv, rs_send, rs_recv):
     tp_size, layers, heads, kc, slots, chunks, seqs = (
         cfg['tp'], cfg['layers'], cfg['heads'], cfg['kc'], cfg['slots'], cfg['chunks'], cfg['seqs'])
@@ -60,7 +61,9 @@
     nope = uk_buf.shape[1]
     keys = ckv_buf.shape[2]
     batch = rows * tp_size
-    n_dq = model // kc
+    ffn = wd_buf.shape[0]
+    half_k = model // 2
+    n_dq = half_k // kc
     cw = model // chunks
     ch = cw // 2
     scale = float((nope + rope) ** -0.5)
@@ -78,21 +81,21 @@
     opp = 2 * ochip + core
 
     barrier = pltpu.get_barrier_semaphore()
-    for peer in (mate, right, left):
+    for peer in (mate, right, left, opp):
         pl.semaphore_signal(barrier, inc=1, device_id={'tp': peer}, device_id_type=MESH)
 
     def x_copy():
         return pltpu.make_async_copy(x_hbm.at[me], xb, x_sem)
 
     def dq_copy(layer, i, slot):
-        off = pl.multiple_of(i * kc, 128)
+        off = pl.multiple_of(core * half_k + i * kc, 128)
         return pltpu.make_async_copy(wdq.at[layer, pl.ds(off, kc), :], dq_buf.at[slot], dq_sem.at[slot])
 
     def kv_copy(layer, i, slot):
-        off = pl.multiple_of(i * kc, 128)
+        off = pl.multiple_of(core * half_k + i * kc, 128)
         return pltpu.make_async_copy(wkv.at[layer, :, pl.ds(off, kc)], kv_buf.at[slot], kv_sem.at[slot])
 
-    weights = [(wuq, uq_buf), (wuk, uk_buf), (wuv, uv_buf), (wo, wo_buf), (wg, wg_buf), (wu, wu_buf), (wd, wd_buf)]
+    weights = [(wuq, uq_buf), (wuk, uk_buf), (wuv, uv_buf), (wo, wo_buf), (wg, wgu_buf.at[0:ffn]), (wu, wgu_buf.at[ffn:2 * ffn]), (wd, wd_buf)]
 
     def w_copy(layer, idx):
         src, dst = weights[idx]
@@ -155,13 +158,19 @@
             ag_start(buf, j, specs[j], 6)
 
         def finish(j):
-            ag_wait(buf, j, specs[j], 3)
-            ag_start(buf, j, specs[j], 7)
-            ag_wait(buf, j, specs[j], 4)
-            ag_start(buf, j, specs[j], 8)
-            for kind in (0, 5, 6, 7, 8):
-                ag_wait(buf, j, specs[j], kind)
-            consume(j)
+            with jax.named_scope('wait_opp'):
+                ag_wait(buf, j, specs[j], 3)
+                ag_start(buf, j, specs[j], 7)
+                ag_wait(buf, j, specs[j], 4)
+                ag_start(buf, j, specs[j], 8)
+            with jax.named_scope('wait_near'):
+                for kind in (0, 5, 6):
+                    ag_wait(buf, j, specs[j], kind)
+            with jax.named_scope('wait_far'):
+                for kind in (7, 8):
+                    ag_wait(buf, j, specs[j], kind)
+            with jax.named_scope('consume'):
+                consume(j)
 
         forward(0)
         for j in range(1, n):
@@ -197,10 +206,11 @@
         def pair(j):
             rs_desc(j, 0).wait_recv()
             cols = pl.ds(j * cw, cw)
-            for cc in range(nchip):
+            psum[ochip, :, cols] = (part[ochip, core, :, cols].astype(F32) + d2d[ochip, :, cols].astype(F32)).astype(BF16)
+            rs_desc(j, 1).start()
+            rs_desc(j, 2).start()
+            for cc in (rchip, lchip, chip):
                 psum[cc, :, cols] = (part[cc, core, :, cols].astype(F32) + d2d[cc, :, cols].astype(F32)).astype(BF16)
-            for kind in (1, 2, 3, 4):
-                rs_desc(j, kind).start()
 
         def combine(j):
             o = j * cw
@@ -219,13 +229,16 @@
             total = psum[chip, :, cols].astype(F32) + fin[0, :, cols].astype(F32) + fin[1, :, cols].astype(F32)
             xb[:, cols] = (xb[:, cols].astype(F32) + total).astype(BF16)
 
-        for j in range(chunks + 2):
+        for j in range(chunks + 1):
             if j < chunks:
                 mm(j)
-            if 0 <= j - 1 < chunks:
+            if j > 0:
                 pair(j - 1)
-            if 0 <= j - 2 < chunks:
-                combine(j - 2)
+        for j in range(chunks):
+            rs_desc(j, 3).start()
+            rs_desc(j, 4).start()
+        for j in range(chunks):
+            combine(j)
         return final
 
     def rs_drain(final):
@@ -246,24 +259,50 @@
             row = jnp.where(layer == i, vals[i:i + 1], row)
         return row
 
+    small = [(pos_hbm, pos_row), (ag_hbm, ag_ref), (mg_hbm, mg_ref), (qg_hbm, qg_ref), (kg_hbm, kg_ref)]
     x_copy().start()
+    for i, (src, dst) in enumerate(small):
+        pltpu.make_async_copy(src, dst, s_sem.at[i]).start()
     start_dq(0)
-    pl.semaphore_wait(barrier, 3)
+    for i, (src, dst) in enumerate(small):
+        pltpu.make_async_copy(src, dst, s_sem.at[i]).wait()
+    pos_f = jnp.transpose(jnp.broadcast_to(pos_row[...].astype(F32), (batch, batch)))
+    pos_ref[...] = pos_f.astype(jnp.int32)
+    lane_f = lax.broadcasted_iota(jnp.int32, (batch, batch), 1) % (rope // 2)
+    angles = pos_f * jnp.exp(lane_f.astype(F32) * (-2.0 * math.log(ROPE_BASE) / rope))
+    cos_v, sin_v = jnp.cos(angles), jnp.sin(angles)
+    lane_s = lax.broadcasted_iota(jnp.int32, (batch, batch), 1) % rope
+    sin_v = jnp.where(lane_s < rope // 2, -sin_v, sin_v)
+    for i in range(heads * rope // batch):
+        cos_ref[:, i * batch:(i + 1) * batch] = cos_v
+        sin_ref[:, i * batch:(i + 1) * batch] = sin_v
     x_copy().wait()
+
+    def pair_copy(src, dst, i):
+        return pltpu.make_async_remote_copy(src_ref=src, dst_ref=dst, send_sem=px_sem.at[0, i], recv_sem=px_sem.at[1, i],
+                                            device_id={'tp': mate}, device_id_type=MESH)
 
     def layer_body(layer, carry):
         more = layer + 1 < layers
         a_buf[...] = rms(xb[...].astype(F32), gain_row(ag_ref, layer)).astype(BF16)
+
+        @pl.when(layer == 0)
+        def _():
+            pl.semaphore_wait(barrier, 4)
+
+        swap = pair_copy(a_buf.at[:, pl.ds(pl.multiple_of(other * half_k, 128), half_k)], a_pair.at[1], 0)
+        swap.start()
+        a_pair[0] = a_buf[:, pl.ds(pl.multiple_of(core * half_k, 128), half_k)]
         acc_q[...] = jnp.zeros_like(acc_q)
-        acc_kv[...] = jnp.zeros_like(acc_kv)
+        swap.wait_recv()
 
         def dq_step(i, c):
             slot = lax.rem(i, slots)
             dq_copy(layer, i, slot).wait()
             kv_copy(layer, i, slot).wait()
-            a_c = a_buf[:, pl.ds(pl.multiple_of(i * kc, 128), kc)]
-            acc_q[...] += dot_nn(a_c, dq_buf[slot])
-            acc_kv[...] += dot_nt(kv_buf[slot], a_c)
+            a_c = a_pair[:, :, pl.ds(pl.multiple_of(i * kc, 128), kc)].reshape(2 * rows, kc)
+            acc_q[:, :, 0:lora] += dot_nn(a_c, dq_buf[slot]).reshape(2, rows, lora)
+            acc_q[:, :, lora:lora + latent + rope] += dot_nt(a_c, kv_buf[slot]).reshape(2, rows, latent + rope)
 
             @pl.when(i + slots < n_dq)
             def _():
@@ -281,8 +320,12 @@
             for idx in (3, 4, 5, 6):
                 w_copy(layer, idx).start()
 
-        q_all[me, :, pl.ds(0, lora)] = rms(acc_q[...], gain_row(qg_ref, layer)).astype(BF16)
-        kv = jnp.transpose(acc_kv[...])
+        back = pair_copy(acc_q.at[1], acc_in, 1)
+        back.start()
+        back.wait_recv()
+        lat = acc_q[0] + acc_in[...]
+        q_all[me, :, pl.ds(0, lora)] = rms(lat[:, :lora], gain_row(qg_ref, layer)).astype(BF16)
+        kv = lat[:, lora:]
         q_all[me, :, pl.ds(lora, latent)] = rms(kv[:, :latent], gain_row(kg_ref, layer)).astype(BF16)
         row0 = pl.multiple_of(me * rows, rows)
         kr = kv[:, latent:latent + rope]
@@ -294,6 +337,8 @@
         def nothing(j):
             return None
 
+        swap.wait_send()
+        back.wait_send()
         all_gather(q_all, q_specs, nothing)
 
         out_c = pltpu.make_async_copy(q_all.at[:, :, pl.ds(lora, latent)], ckv_out.at[layer], out_sem.at[0])
@@ -336,14 +381,11 @@
             cache = ckv_buf[slot].reshape(seqs * keys, latent)
             u_g = u_buf[:, pl.ds(r0, seqs), :].reshape(m_rows, latent)
             r_g = r_buf[:, pl.ds(r0, seqs), :].reshape(m_rows, 2 * rope).astype(F32)
-            u_2 = jnp.concatenate([u_g, u_g], axis=0)
-            s_t = dot_nt(cache, u_2)
-            lane_t = lax.broadcasted_iota(jnp.int32, (keys, 2 * m_rows), 1) % seqs
-            sel = s_t[0:keys]
+            row_b = lax.broadcasted_iota(jnp.int32, (m_rows, keys), 0) % seqs
+            s_t = dot_nt(u_g, cache)
+            s_n = s_t[:, 0:keys]
             for b in range(1, seqs):
-                sel = jnp.where(lane_t == b, s_t[b * keys:(b + 1) * keys], sel)
-            s_n = jnp.transpose(sel)[0:m_rows]
-            row_b = lax.broadcasted_iota(jnp.int32, (m_rows, keys), 0) % seqs
+                s_n = jnp.where(row_b == b, s_t[:, b * keys:(b + 1) * keys], s_n)
             lane_k = lax.broadcasted_iota(jnp.int32, (m_rows, keys), 1)
             row_r = lax.broadcasted_iota(jnp.int32, (m_rows, 2 * rope), 0) % seqs
             lane_r = lax.broadcasted_iota(jnp.int32, (m_rows, 2 * rope), 1) // rope
@@ -404,18 +446,15 @@
         def gate_up(j):
             cols = pl.ds(j * cw, cw)
             b_c = b_all[:, :, cols].reshape(batch, cw)
-            g_v = dot_nt(wg_buf[:, cols], b_c)
-            u_v = dot_nt(wu_buf[:, cols], b_c)
+            val = dot_nt(b_c, wgu_buf[:, cols])
             if j == 0:
-                gate_acc[...] = g_v
-                up_acc[...] = u_v
+                gu_acc[...] = val
             else:
-                gate_acc[...] += g_v
-                up_acc[...] += u_v
+                gu_acc[...] += val
 
         all_gather(b_all, b_specs, gate_up)
-        gate = gate_acc[...]
-        act_buf[...] = jnp.transpose(gate * lax.logistic(gate) * up_acc[...]).astype(BF16)
+        gate = gu_acc[:, 0:ffn]
+        act_buf[...] = (gate * lax.logistic(gate) * gu_acc[:, ffn:2 * ffn]).astype(BF16)
         w_copy(layer, 6).wait()
 
         @pl.when(more)
@@ -465,34 +504,32 @@
         ffn = w_gate.shape[-1]
         rows = batch // tp
         kc, slots, chunks, seqs = 512, 4, 4, rows
-        half = rope // 2
-
-        inv_freq = jnp.exp(jnp.arange(half, dtype=F32) * (-2.0 * math.log(ROPE_BASE) / rope))
-        angles = pos_ids.astype(F32)[:, None] * inv_freq
-        cos, sin = jnp.cos(angles), jnp.sin(angles)
-        cos_t = jnp.tile(jnp.concatenate([cos, cos], axis=1), (1, heads))
-        sin_t = jnp.tile(jnp.concatenate([-sin, sin], axis=1), (1, heads))
-        pos_t = jnp.broadcast_to(pos_ids[:, None], (batch, keys))
-
-        vm = pl.BlockSpec(memory_space=pltpu.VMEM)
         hb = pl.BlockSpec(memory_space=pl.ANY)
         dma = pltpu.SemaphoreType.DMA
         qw = lora + latent + 2 * rope
         ch = model // chunks // 2
         scratch = [
+            pltpu.VMEM((1, batch), jnp.int32),
+            pltpu.VMEM((layers, model), BF16),
+            pltpu.VMEM((layers, model), BF16),
+            pltpu.VMEM((layers, lora), BF16),
+            pltpu.VMEM((layers, latent), BF16),
+            pltpu.VMEM((batch, heads * rope), F32),
+            pltpu.VMEM((batch, heads * rope), F32),
+            pltpu.VMEM((batch, keys), jnp.int32),
             pltpu.VMEM((rows, model), BF16),
             pltpu.VMEM((rows, model), BF16),
+            pltpu.VMEM((2, rows, model // 2), BF16),
+            pltpu.VMEM((rows, lora + latent + 2 * rope), F32),
             pltpu.VMEM((tp, rows, model), BF16),
             pltpu.VMEM((tp, rows, qw), BF16),
-            pltpu.VMEM((rows, lora), F32),
-            pltpu.VMEM((latent + rope, rows), F32),
+            pltpu.VMEM((2, rows, lora + latent + 2 * rope), F32),
             pltpu.VMEM((heads, batch, latent), BF16),
             pltpu.VMEM((heads, batch, 2 * rope), BF16),
             pltpu.VMEM((heads, batch, latent), BF16),
             pltpu.VMEM((batch, heads * nope), BF16),
             pltpu.VMEM((latent * heads, nope), F32),
-            pltpu.VMEM((ffn, batch), F32),
-            pltpu.VMEM((ffn, batch), F32),
+            pltpu.VMEM((batch, 2 * ffn), F32),
             pltpu.VMEM((batch, ffn), BF16),
             pltpu.VMEM((tp // 2, 2, rows, model), BF16),
             pltpu.VMEM((tp // 2, rows, model), BF16),
@@ -506,12 +543,11 @@
             pltpu.VMEM((latent * heads, nope), BF16),
             pltpu.VMEM((latent * heads, nope), BF16),
             pltpu.VMEM((heads * nope, model), BF16),
-            pltpu.VMEM((ffn, model), BF16),
-            pltpu.VMEM((ffn, model), BF16),
+            pltpu.VMEM((2 * ffn, model), BF16),
             pltpu.VMEM((ffn, model), BF16),
             pltpu.VMEM((2, seqs, keys, latent), BF16),
             pltpu.VMEM((2, seqs, rope, keys), BF16),
-            dma(()), dma((slots,)), dma((slots,)), dma((7,)), dma((2, 2)), dma((max(chunks, 2),)),
+            dma(()), dma((5,)), dma((2, 2)), dma((slots,)), dma((slots,)), dma((7,)), dma((2, 2)), dma((max(chunks, 2),)),
             dma((chunks, 9)), dma((chunks, 9)), dma((chunks, 7)), dma((chunks, 7)),
         ]
         cfg = dict(tp=tp, layers=layers, heads=heads, kc=kc, slots=slots, chunks=chunks, seqs=seqs)
@@ -520,14 +556,14 @@
             out_shape=(jax.ShapeDtypeStruct((tp, rows, model), BF16),
                        jax.ShapeDtypeStruct((layers, tp, rows, latent), BF16),
                        jax.ShapeDtypeStruct((layers, tp, rows, 2 * rope), BF16)),
-            in_specs=[hb, vm, vm, vm, vm, vm, vm, vm] + [hb] * 11,
+            in_specs=[hb] * 17,
             out_specs=(hb, hb, hb),
             scratch_shapes=scratch,
             compiler_params=pltpu.CompilerParams(collective_id=0, has_side_effects=True, vmem_limit_bytes=67043328),
             name='decode_step',
         )
         x_o, c_o, k_o = call(
-            x_in.reshape(tp, rows, model), cos_t, sin_t, pos_t, attn_gain, mlp_gain, q_gain, kv_gain,
+            x_in.reshape(tp, rows, model), pos_ids.reshape(1, batch), attn_gain, mlp_gain, q_gain, kv_gain,
             w_dq, w_dkv.transpose(0, 2, 1), w_uq.transpose(0, 2, 3, 1).reshape(layers, heads * per, lora),
             w_uk.reshape(layers, latent * heads, nope), w_uv.reshape(layers, latent * heads, nope),
             w_o.reshape(layers, heads * nope, model),

time: 197 us -> 176 us (0.89)
  Pallas kernels: 186 us -> 169 us
  local copies, waits for them, and re-layouts: 8.96 us -> 6.06 us
    pallas_call x1, Pallas kernels: 186 us -> 169 us  [device_body(): call(x_in.reshape(tp, rows, model), pos_ids.reshape(1, batch), attn_gain,...]
where the time goes in v2:
time: 176 us; the launch traced here: 175 us
  Pallas kernels  169 us (96%)
  local copies, waits for them, and re-layouts  6.06 us (3%)
    pallas_call x1, Pallas kernels, device_body(): call(x_in.reshape(tp, rows, model), pos_ids.reshape(1, batch), attn_gain,...  169 us
    unnamed x3, local copies, waits for them, and re-layouts  6.06 us

profile of v2, /device:TPU:113, one launch (start us, length us, event | category | flops | bytes accessed | tf_op | source)
XLA Modules:
  0.0 175.3 jit_solution(8153230267921240114)
XLA Ops:
  0.6 168.6 %decode_step.1 = (bf16[8,16,7168]{2,1,0:T(8,128)(2,1)}, bf16[2,8,16,512]{3,2,1,0:T(8,128)(2,1)}, bf16[2,8,16,128]{3,2,1,0:T(8,128)(2,1)}) custom-call(bf16[8,16,7168]{2,1,0:T(8,128)(2,1)} %bitcast.22, s32[1,128]{1,0:T(1,128)} %bitcast.28, bf16[2,7168]{1,0:T(2,128)(2,1)} %ag_hbm.1, bf16[2,7168]{1,0:T(2,128)(2,1)} %mg_hbm.1, bf16[2,1536]{1,0:T(2,128)(2,1)} %qg_hbm.1, ...), custom_call_target="tpu_custom_call" | custom-call | tf_op jit(solution)/shard_map/decode_step/pallas_call | solution.py:565
  169.2 1.5 copy.21
  170.7 2.8 %copy.24 = bf16[128,7168]{1,0:T(8,128)(2,1)} copy(bf16[128,7168]{1,0:T(8,128)(2,1)} %bitcast.23) | data formatting | bytes 3670016
  173.6 1.7 copy.25

commit v3 on v2

--- a/solution.py
+++ b/solution.py
@@ -47,7 +47,7 @@
                 xb, a_buf, a_pair, acc_in, b_all, q_all, acc_q, u_buf, r_buf, ctx_buf, o_buf, wf,
                 gu_acc, act_buf,
                 part, d2d, psum, rel, cmb, fin,
-                dq_buf, kv_buf, uq_buf, uk_buf, uv_buf, wo_buf, wgu_buf, wd_buf, ckv_buf, kpe_buf,
+                dq_buf, kv_buf, uq_buf, uk_buf, uv_buf, wo_buf, wgu_buf, wd_buf, ckv_buf, kpe_buf, s_buf,
                 x_sem, s_sem, px_sem, dq_sem, kv_sem, w_sem, c_sem, out_sem,
                 ag_send, ag_recv, rs_send, rs_recv):
     tp_size, layers, heads, kc, slots, chunks, seqs = (
@@ -62,6 +62,7 @@
     keys = ckv_buf.shape[2]
     batch = rows * tp_size
     ffn = wd_buf.shape[0]
+    cslots = cfg['cslots']
     half_k = model // 2
     n_dq = half_k // kc
     cw = model // chunks
@@ -113,7 +114,7 @@
             kv_copy(layer, s, s).start()
 
     def start_cache(layer):
-        for s in range(2):
+        for s in range(cslots):
             ckv_copy(layer, s, s).start()
             kpe_copy(layer, s, s).start()
 
@@ -122,11 +123,11 @@
                                             recv_sem=recvs.at[j, kind], device_id={'tp': dev}, device_id_type=MESH)
 
     def ag_desc(buf, j, spec, kind, blk, dev):
-        off, half_a, width = spec
+        off, half_a, width, direct = spec
         lo, size = off, width
-        if kind in (3, 7):
+        if not direct and kind in (3, 7):
             size = half_a
-        elif kind in (4, 8):
+        elif not direct and kind in (4, 8):
             lo, size = off + half_a, width - half_a
         ref = buf.at[blk, :, pl.ds(lo, size)]
         return remote(ref, ref, ag_send, ag_recv, j, kind, dev)
@@ -137,8 +138,13 @@
     ag_out = [(me, mate), (me, right), (me, left), (left, right), (right, left), (left, mate), (right, mate), (opp, mate), (opp, mate)]
     ag_in = [mate, left, right, opp, opp, mleft, mright, mopp, mopp]
 
+    def ag_route(spec, kind):
+        if kind == 3 and spec[3]:
+            return me, opp
+        return ag_out[kind]
+
     def ag_start(buf, j, spec, kind):
-        ag_desc(buf, j, spec, kind, *ag_out[kind]).start()
+        ag_desc(buf, j, spec, kind, *ag_route(spec, kind)).start()
 
     def ag_wait(buf, j, spec, kind):
         ag_desc(buf, j, spec, kind, ag_in[kind], mate).wait_recv()
@@ -146,40 +152,49 @@
     def all_gather(buf, specs, consume):
         n = len(specs)
         for j in range(n):
-            for kind in (1, 2, 0):
+            for kind in ((1, 2, 3, 0) if specs[j][3] else (1, 2, 0)):
                 ag_start(buf, j, specs[j], kind)
 
         def forward(j):
-            ag_wait(buf, j, specs[j], 1)
-            ag_start(buf, j, specs[j], 3)
-            ag_start(buf, j, specs[j], 5)
-            ag_wait(buf, j, specs[j], 2)
-            ag_start(buf, j, specs[j], 4)
-            ag_start(buf, j, specs[j], 6)
+            direct = specs[j][3]
+            for kind in (1, 2):
+                ag_wait(buf, j, specs[j], kind)
+                if not direct:
+                    ag_start(buf, j, specs[j], kind + 2)
+                ag_start(buf, j, specs[j], kind + 4)
+
+        def pass_far(j):
+            for kind in ((3,) if specs[j][3] else (3, 4)):
+                ag_wait(buf, j, specs[j], kind)
+                ag_start(buf, j, specs[j], kind + 4)
 
         def finish(j):
-            with jax.named_scope('wait_opp'):
-                ag_wait(buf, j, specs[j], 3)
-                ag_start(buf, j, specs[j], 7)
-                ag_wait(buf, j, specs[j], 4)
-                ag_start(buf, j, specs[j], 8)
-            with jax.named_scope('wait_near'):
-                for kind in (0, 5, 6):
-                    ag_wait(buf, j, specs[j], kind)
-            with jax.named_scope('wait_far'):
-                for kind in (7, 8):
-                    ag_wait(buf, j, specs[j], kind)
+            for kind in ((0, 5, 6, 7) if specs[j][3] else (0, 5, 6, 7, 8)):
+                ag_wait(buf, j, specs[j], kind)
             with jax.named_scope('consume'):
                 consume(j)
 
-        forward(0)
-        for j in range(1, n):
+        lead = sum(spec[3] for spec in specs)
+        if n == 1:
+            lead = 0
+        for j in range(n):
             forward(j)
-            finish(j - 1)
-        finish(n - 1)
+            if 1 <= j <= lead:
+                pass_far(j - 1)
+            if 2 <= j <= lead + 1:
+                finish(j - 2)
+        if lead:
+            for j in range(max(n - 2, 0), lead):
+                finish(j)
+        pass_far(lead)
+        for j in range(lead, n):
+            if j + 1 < n:
+                pass_far(j + 1)
+            finish(j)
         for j in range(n):
             for kind in range(9):
-                ag_desc(buf, j, specs[j], kind, *ag_out[kind]).wait_send()
+                if not (specs[j][3] and kind in (4, 8)):
+                    ag_desc(buf, j, specs[j], kind, *ag_route(specs[j], kind)).wait_send()
 
     def rs_desc(j, kind):
         o = j * cw
@@ -248,9 +263,13 @@
             for kind in range(7):
                 rs_desc(j, kind).wait_send()
 
-    b_specs = [(j * cw, ch, cw) for j in range(chunks)]
+    gchunks = cfg['gchunks']
+    gw = model // gchunks
+    gh = (gw // 128 + 1) // 2 * 128
+    b_specs = [(j * gw, gh, gw, j < cfg['direct']) for j in range(gchunks)]
+    x_specs = [(j * gw, gh, gw, False) for j in range(gchunks)]
     qw = q_all.shape[2]
-    q_specs = [(0, (qw // 256 + 1) * 128 if (qw // 128) % 2 else qw // 2, qw)]
+    q_specs = [(0, 0, qw, True)]
 
     def gain_row(ref, layer):
         vals = ref[...].astype(F32)
@@ -317,8 +336,7 @@
             for idx in (0, 1, 2):
                 w_copy(layer, idx).start()
             start_cache(layer)
-            for idx in (3, 4, 5, 6):
-                w_copy(layer, idx).start()
+            w_copy(layer, 3).start()
 
         back = pair_copy(acc_q.at[1], acc_in, 1)
         back.start()
@@ -373,47 +391,73 @@
 
         m_rows = heads * seqs
 
-        def att_step(g, c):
-            slot = lax.rem(g, 2)
+        groups = batch // seqs
+        row_b = lax.broadcasted_iota(jnp.int32, (m_rows, keys), 0) % seqs
+        lane_k = lax.broadcasted_iota(jnp.int32, (m_rows, keys), 1)
+        lane_r = lax.broadcasted_iota(jnp.int32, (m_rows, 2 * rope), 1) // rope
+
+        def att_wait(g):
+            slot = lax.rem(g, cslots)
             ckv_copy(layer, g, slot).wait()
             kpe_copy(layer, g, slot).wait()
+
+        def scores(g):
+            slot = lax.rem(g, cslots)
             r0 = pl.multiple_of(g * seqs, seqs)
-            cache = ckv_buf[slot].reshape(seqs * keys, latent)
             u_g = u_buf[:, pl.ds(r0, seqs), :].reshape(m_rows, latent)
             r_g = r_buf[:, pl.ds(r0, seqs), :].reshape(m_rows, 2 * rope).astype(F32)
-            row_b = lax.broadcasted_iota(jnp.int32, (m_rows, keys), 0) % seqs
-            s_t = dot_nt(u_g, cache)
+            s_t = dot_nt(u_g, ckv_buf[slot].reshape(seqs * keys, latent))
             s_n = s_t[:, 0:keys]
             for b in range(1, seqs):
                 s_n = jnp.where(row_b == b, s_t[:, b * keys:(b + 1) * keys], s_n)
-            lane_k = lax.broadcasted_iota(jnp.int32, (m_rows, keys), 1)
-            row_r = lax.broadcasted_iota(jnp.int32, (m_rows, 2 * rope), 0) % seqs
-            lane_r = lax.broadcasted_iota(jnp.int32, (m_rows, 2 * rope), 1) // rope
             q_blk = jnp.concatenate(
-                [jnp.where(row_r == 2 * b + lane_r, r_g, 0.0).astype(BF16) for b in range(seqs // 2)], axis=1)
+                [jnp.where(row_b == 2 * b + lane_r, r_g, 0.0).astype(BF16) for b in range(seqs // 2)], axis=1)
             s_r = dot_nn(q_blk, kpe_buf[slot].reshape(seqs * rope, keys))
             cn = tile_rows(q_all[g, :, pl.ds(lora, latent)].astype(F32), heads)
             kn = tile_rows(q_all[g, :, pl.ds(lora + latent, 2 * rope)].astype(F32), heads)
             fresh = jnp.sum(u_g.astype(F32) * cn, axis=-1, keepdims=True) + jnp.sum(r_g * kn, axis=-1, keepdims=True)
             pos = tile_rows(pos_ref[pl.ds(r0, seqs), :], heads)
-            at_pos = lane_k == pos
-            s = jnp.where(at_pos, fresh, s_n + s_r) * scale
-            s = jnp.where(lane_k <= pos, s, NEG_INF)
+            s = jnp.where(lane_k == pos, fresh, s_n + s_r) * scale
+            return jnp.where(lane_k <= pos, s, NEG_INF)
+
+        def context(g, s):
+            slot = lax.rem(g, cslots)
+            r0 = pl.multiple_of(g * seqs, seqs)
             e = jnp.exp(s - jnp.max(s, axis=-1, keepdims=True))
             prob = (e / jnp.sum(e, axis=-1, keepdims=True)).astype(BF16).astype(F32)
+            at_pos = lane_k == tile_rows(pos_ref[pl.ds(r0, seqs), :], heads)
             p_new = jnp.sum(jnp.where(at_pos, prob, 0.0), axis=-1, keepdims=True)
             p_old = jnp.where(at_pos, 0.0, prob)
             p_blk = jnp.concatenate([jnp.where(row_b == b, p_old, 0.0).astype(BF16) for b in range(seqs)], axis=1)
-            ctx = dot_nn(p_blk, cache) + p_new * cn
+            cn = tile_rows(q_all[g, :, pl.ds(lora, latent)].astype(F32), heads)
+            ctx = dot_nn(p_blk, ckv_buf[slot].reshape(seqs * keys, latent)) + p_new * cn
             ctx_buf[:, pl.ds(r0, seqs), :] = ctx.astype(BF16).reshape(heads, seqs, latent)
 
-            @pl.when(g + 2 < batch // seqs)
+        att_wait(0)
+        s_buf[...] = scores(0)
+
+        def att_step(g, c):
+            att_wait(g + 1)
+            s_now = s_buf[...]
+            s_next = scores(g + 1)
+            context(g, s_now)
+            s_buf[...] = s_next
+
+            @pl.when(g + cslots < groups)
             def _():
-                ckv_copy(layer, g + 2, slot).start()
-                kpe_copy(layer, g + 2, slot).start()
+                slot = lax.rem(g, cslots)
+                ckv_copy(layer, g + cslots, slot).start()
+                kpe_copy(layer, g + cslots, slot).start()
             return c
 
-        lax.fori_loop(0, batch // seqs, att_step, 0)
+        lax.fori_loop(0, groups - 1, att_step, 0)
+
+        @pl.when(layer == 0)
+        def _():
+            for idx in (4, 5, 6):
+                w_copy(layer, idx).start()
+
+        context(groups - 1, s_buf[...])
 
         w_copy(layer, 2).wait()
         wf[...] = uv_buf[...].astype(F32)
@@ -444,8 +488,8 @@
         w_copy(layer, 5).wait()
 
         def gate_up(j):
-            cols = pl.ds(j * cw, cw)
-            b_c = b_all[:, :, cols].reshape(batch, cw)
+            cols = pl.ds(j * gw, gw)
+            b_c = b_all[:, :, cols].reshape(batch, gw)
             val = dot_nt(b_c, wgu_buf[:, cols])
             if j == 0:
                 gu_acc[...] = val
@@ -476,12 +520,12 @@
     b_all[me] = xb[...]
 
     def put(j):
-        cols = pl.ds(j * cw, cw)
+        cols = pl.ds(j * gw, gw)
         pltpu.make_async_copy(b_all.at[:, :, cols], x_out.at[:, :, cols], out_sem.at[j]).start()
 
-    all_gather(b_all, b_specs, put)
-    for j in range(chunks):
-        cols = pl.ds(j * cw, cw)
+    all_gather(b_all, x_specs, put)
+    for j in range(gchunks):
+        cols = pl.ds(j * gw, gw)
         pltpu.make_async_copy(b_all.at[:, :, cols], x_out.at[:, :, cols], out_sem.at[j]).wait()
 
 
@@ -503,7 +547,7 @@
         nope = w_uk.shape[-1]
         ffn = w_gate.shape[-1]
         rows = batch // tp
-        kc, slots, chunks, seqs = 512, 4, 4, rows
+        kc, slots, chunks, gchunks, direct, seqs, cslots = 512, 3, 4, 4, 1, rows, 3
         hb = pl.BlockSpec(memory_space=pl.ANY)
         dma = pltpu.SemaphoreType.DMA
         qw = lora + latent + 2 * rope
@@ -545,12 +589,13 @@
             pltpu.VMEM((heads * nope, model), BF16),
             pltpu.VMEM((2 * ffn, model), BF16),
             pltpu.VMEM((ffn, model), BF16),
-            pltpu.VMEM((2, seqs, keys, latent), BF16),
-            pltpu.VMEM((2, seqs, rope, keys), BF16),
-            dma(()), dma((5,)), dma((2, 2)), dma((slots,)), dma((slots,)), dma((7,)), dma((2, 2)), dma((max(chunks, 2),)),
-            dma((chunks, 9)), dma((chunks, 9)), dma((chunks, 7)), dma((chunks, 7)),
+            pltpu.VMEM((cslots, seqs, keys, latent), BF16),
+            pltpu.VMEM((cslots, seqs, rope, keys), BF16),
+            pltpu.VMEM((heads * seqs, keys), F32),
+            dma(()), dma((5,)), dma((2, 2)), dma((slots,)), dma((slots,)), dma((7,)), dma((2, cslots)), dma((gchunks,)),
+            dma((gchunks, 9)), dma((gchunks, 9)), dma((chunks, 7)), dma((chunks, 7)),
         ]
-        cfg = dict(tp=tp, layers=layers, heads=heads, kc=kc, slots=slots, chunks=chunks, seqs=seqs)
+        cfg = dict(tp=tp, layers=layers, heads=heads, kc=kc, slots=slots, chunks=chunks, seqs=seqs, cslots=cslots, gchunks=gchunks, direct=direct)
         call = pl.pallas_call(
             functools.partial(step_kernel, cfg),
             out_shape=(jax.ShapeDtypeStruct((tp, rows, model), BF16),

time: 176 us -> 161 us (0.915)
  Pallas kernels: 169 us -> 153 us
    pallas_call x1, Pallas kernels: 169 us -> 153 us  [device_body(): call(x_in.reshape(tp, rows, model), pos_ids.reshape(1, batch), attn_gain,...]
where the time goes in v3:
time: 161 us; the launch traced here: 160 us
  Pallas kernels  153 us (95%)
  local copies, waits for them, and re-layouts  6.06 us (4%)
    pallas_call x1, Pallas kernels, device_body(): call(x_in.reshape(tp, rows, model), pos_ids.reshape(1, batch), attn_gain,...  153 us
    unnamed x3, local copies, waits for them, and re-layouts  6.06 us

profile of v3, /device:TPU:113, one launch (start us, length us, event | category | flops | bytes accessed | tf_op | source)
XLA Modules:
  0.0 160.1 jit_solution(1192834328803622492)
XLA Ops:
  0.6 153.4 %decode_step.1 = (bf16[8,16,7168]{2,1,0:T(8,128)(2,1)}, bf16[2,8,16,512]{3,2,1,0:T(8,128)(2,1)}, bf16[2,8,16,128]{3,2,1,0:T(8,128)(2,1)}) custom-call(bf16[8,16,7168]{2,1,0:T(8,128)(2,1)} %bitcast.22, s32[1,128]{1,0:T(1,128)} %bitcast.28, bf16[2,7168]{1,0:T(2,128)(2,1)} %ag_hbm.1, bf16[2,7168]{1,0:T(2,128)(2,1)} %mg_hbm.1, bf16[2,1536]{1,0:T(2,128)(2,1)} %qg_hbm.1, ...), custom_call_target="tpu_custom_call" | custom-call | tf_op jit(solution)/shard_map/decode_step/pallas_call | solution.py:610
  154.0 1.5 copy.21
  155.6 2.8 %copy.24 = bf16[128,7168]{1,0:T(8,128)(2,1)} copy(bf16[128,7168]{1,0:T(8,128)(2,1)} %bitcast.23) | data formatting | bytes 3670016
  158.4 1.7 %copy.25 = bf16[2,128,512]{2,1,0:T(8,128)(2,1)} copy(bf16[2,128,512]{2,1,0:T(8,128)(2,1)} %bitcast.26) | data formatting | bytes 524288

commit v4 on v3

--- a/solution.py
+++ b/solution.py
@@ -44,11 +44,11 @@
                 wdq, wkv, wuq, wuk, wuv, wo, wg, wu, wd, ckv_hbm, kpe_hbm,
                 x_out, ckv_out, kpe_out,
                 pos_row, ag_ref, mg_ref, qg_ref, kg_ref, cos_ref, sin_ref, pos_ref,
-                xb, a_buf, a_pair, acc_in, b_all, q_all, acc_q, u_buf, r_buf, ctx_buf, o_buf, wf,
+                xb, a_buf, a_pair, acc_in, b_all, q_all, acc_q, acc_all, acc_rcv, u_buf, r_buf, u_in, r_in, ctx_buf, ctx_out, o_buf, wf,
                 gu_acc, act_buf,
                 part, d2d, psum, rel, cmb, fin,
                 dq_buf, kv_buf, uq_buf, uk_buf, uv_buf, wo_buf, wgu_buf, wd_buf, ckv_buf, kpe_buf, s_buf,
-                x_sem, s_sem, px_sem, dq_sem, kv_sem, w_sem, c_sem, out_sem,
+                x_sem, s_sem, px_sem, hx_sem, cx_sem, dq_sem, kv_sem, w_sem, c_sem, out_sem,
                 ag_send, ag_recv, rs_send, rs_recv):
     tp_size, layers, heads, kc, slots, chunks, seqs = (
         cfg['tp'], cfg['layers'], cfg['heads'], cfg['kc'], cfg['slots'], cfg['chunks'], cfg['seqs'])
@@ -86,7 +86,7 @@
         pl.semaphore_signal(barrier, inc=1, device_id={'tp': peer}, device_id_type=MESH)
 
     def x_copy():
-        return pltpu.make_async_copy(x_hbm.at[me], xb, x_sem)
+        return pltpu.make_async_copy(x_hbm.at[me], xb, x_sem.at[0])
 
     def dq_copy(layer, i, slot):
         off = pl.multiple_of(core * half_k + i * kc, 128)
@@ -103,10 +103,10 @@
         return pltpu.make_async_copy(src.at[layer], dst, w_sem.at[idx])
 
     def ckv_copy(layer, g, slot):
-        return pltpu.make_async_copy(ckv_hbm.at[layer, pl.ds(g * seqs, seqs)], ckv_buf.at[slot], c_sem.at[0, slot])
+        return pltpu.make_async_copy(ckv_hbm.at[layer, pl.ds(core * (batch // 2) + g * seqs, seqs)], ckv_buf.at[slot], c_sem.at[0, slot])
 
     def kpe_copy(layer, g, slot):
-        return pltpu.make_async_copy(kpe_hbm.at[layer, pl.ds(g * seqs, seqs)], kpe_buf.at[slot], c_sem.at[1, slot])
+        return pltpu.make_async_copy(kpe_hbm.at[layer, pl.ds(core * (batch // 2) + g * seqs, seqs)], kpe_buf.at[slot], c_sem.at[1, slot])
 
     def start_dq(layer):
         for s in range(slots):
@@ -149,11 +149,15 @@
     def ag_wait(buf, j, spec, kind):
         ag_desc(buf, j, spec, kind, ag_in[kind], mate).wait_recv()
 
-    def all_gather(buf, specs, consume):
+    def ag_first(buf, j, spec):
+        for kind in ((1, 2, 3, 0) if spec[3] else (1, 2, 0)):
+            ag_start(buf, j, spec, kind)
+
+    def all_gather(buf, specs, consume, started=False):
         n = len(specs)
         for j in range(n):
-            for kind in ((1, 2, 3, 0) if specs[j][3] else (1, 2, 0)):
-                ag_start(buf, j, specs[j], kind)
+            if not started:
+                ag_first(buf, j, specs[j])
 
         def forward(j):
             direct = specs[j][3]
@@ -256,9 +260,11 @@
             combine(j)
         return final
 
-    def rs_drain(final):
+    def rs_drain(final, hook=None):
         for j in range(chunks):
             final(j)
+            if hook is not None:
+                hook(j)
         for j in range(chunks):
             for kind in range(7):
                 rs_desc(j, kind).wait_send()
@@ -267,7 +273,7 @@
     gw = model // gchunks
     gh = (gw // 128 + 1) // 2 * 128
     b_specs = [(j * gw, gh, gw, j < cfg['direct']) for j in range(gchunks)]
-    x_specs = [(j * gw, gh, gw, False) for j in range(gchunks)]
+    x_specs = [(j * cw, ch, cw, False) for j in range(chunks)]
     qw = q_all.shape[2]
     q_specs = [(0, 0, qw, True)]
 
@@ -279,6 +285,8 @@
         return row
 
     small = [(pos_hbm, pos_row), (ag_hbm, ag_ref), (mg_hbm, mg_ref), (qg_hbm, qg_ref), (kg_hbm, kg_ref)]
+    x_all = pltpu.make_async_copy(x_hbm, b_all, x_sem.at[1])
+    x_all.start()
     x_copy().start()
     for i, (src, dst) in enumerate(small):
         pltpu.make_async_copy(src, dst, s_sem.at[i]).start()
@@ -301,27 +309,25 @@
         return pltpu.make_async_remote_copy(src_ref=src, dst_ref=dst, send_sem=px_sem.at[0, i], recv_sem=px_sem.at[1, i],
                                             device_id={'tp': mate}, device_id_type=MESH)
 
-    def layer_body(layer, carry):
-        more = layer + 1 < layers
-        a_buf[...] = rms(xb[...].astype(F32), gain_row(ag_ref, layer)).astype(BF16)
-
-        @pl.when(layer == 0)
-        def _():
-            pl.semaphore_wait(barrier, 4)
-
-        swap = pair_copy(a_buf.at[:, pl.ds(pl.multiple_of(other * half_k, 128), half_k)], a_pair.at[1], 0)
-        swap.start()
-        a_pair[0] = a_buf[:, pl.ds(pl.multiple_of(core * half_k, 128), half_k)]
-        acc_q[...] = jnp.zeros_like(acc_q)
-        swap.wait_recv()
-
+    def put_latents(layer, blk, lat):
+        q_all[blk, :, pl.ds(0, lora)] = rms(lat[:, :lora], gain_row(qg_ref, layer)).astype(BF16)
+        kv = lat[:, lora:]
+        q_all[blk, :, pl.ds(lora, latent)] = rms(kv[:, :latent], gain_row(kg_ref, layer)).astype(BF16)
+        row0 = pl.multiple_of(blk * rows, rows)
+        kr = kv[:, latent:latent + rope]
+        kr = jnp.concatenate([kr, kr], axis=1)
+        kr = kr * cos_ref[pl.ds(row0, rows), 0:2 * rope] + swap_halves(kr, rope // 2) * sin_ref[pl.ds(row0, rows), 0:2 * rope]
+        lane = lax.broadcasted_iota(jnp.int32, kr.shape, 1)
+        q_all[blk, :, pl.ds(lora + latent, 2 * rope)] = jnp.where(lane < rope, kr, 0.0).astype(BF16)
+
+    def down_project(layer, blocks, acts, acc):
         def dq_step(i, c):
             slot = lax.rem(i, slots)
             dq_copy(layer, i, slot).wait()
             kv_copy(layer, i, slot).wait()
-            a_c = a_pair[:, :, pl.ds(pl.multiple_of(i * kc, 128), kc)].reshape(2 * rows, kc)
-            acc_q[:, :, 0:lora] += dot_nn(a_c, dq_buf[slot]).reshape(2, rows, lora)
-            acc_q[:, :, lora:lora + latent + rope] += dot_nt(a_c, kv_buf[slot]).reshape(2, rows, latent + rope)
+            a_c = acts(i)
+            acc[:, :, 0:lora] += dot_nn(a_c, dq_buf[slot]).reshape(blocks, rows, lora)
+            acc[:, :, lora:lora + latent + rope] += dot_nt(a_c, kv_buf[slot]).reshape(blocks, rows, latent + rope)
 
             @pl.when(i + slots < n_dq)
             def _():
@@ -331,38 +337,65 @@
 
         lax.fori_loop(0, n_dq, dq_step, 0)
 
-        @pl.when(layer == 0)
-        def _():
-            for idx in (0, 1, 2):
-                w_copy(layer, idx).start()
-            start_cache(layer)
-            w_copy(layer, 3).start()
-
-        back = pair_copy(acc_q.at[1], acc_in, 1)
-        back.start()
-        back.wait_recv()
-        lat = acc_q[0] + acc_in[...]
-        q_all[me, :, pl.ds(0, lora)] = rms(lat[:, :lora], gain_row(qg_ref, layer)).astype(BF16)
-        kv = lat[:, lora:]
-        q_all[me, :, pl.ds(lora, latent)] = rms(kv[:, :latent], gain_row(kg_ref, layer)).astype(BF16)
-        row0 = pl.multiple_of(me * rows, rows)
-        kr = kv[:, latent:latent + rope]
-        kr = jnp.concatenate([kr, kr], axis=1)
-        kr = kr * cos_ref[pl.ds(row0, rows), 0:2 * rope] + swap_halves(kr, rope // 2) * sin_ref[pl.ds(row0, rows), 0:2 * rope]
-        lane = lax.broadcasted_iota(jnp.int32, kr.shape, 1)
-        q_all[me, :, pl.ds(lora + latent, 2 * rope)] = jnp.where(lane < rope, kr, 0.0).astype(BF16)
-
-        def nothing(j):
-            return None
-
-        swap.wait_send()
-        back.wait_send()
-        all_gather(q_all, q_specs, nothing)
-
+    x_all.wait()
+    gain_0 = ag_ref[0:1, :].astype(F32)
+
+    def norm_block(i, c):
+        b_all[i] = rms(b_all[i].astype(F32), gain_0).astype(BF16)
+        return c
+
+    lax.fori_loop(0, tp_size, norm_block, 0)
+    acc_all[...] = jnp.zeros_like(acc_all)
+    down_project(0, tp_size, lambda i: b_all[:, :, pl.ds(pl.multiple_of(core * half_k + i * kc, 128), kc)].reshape(batch, kc), acc_all)
+    for idx in (0, 1, 2):
+        w_copy(0, idx).start()
+    start_cache(0)
+    w_copy(0, 3).start()
+    pl.semaphore_wait(barrier, 4)
+    whole = pair_copy(acc_all, acc_rcv, 2)
+    whole.start()
+    whole.wait_recv()
+
+    def latent_block(i, c):
+        put_latents(0, i, acc_all[i] + acc_rcv[i])
+        return c
+
+    lax.fori_loop(0, tp_size, latent_block, 0)
+    whole.wait_send()
+
+    def front(layer):
+        with jax.named_scope('norm'):
+            a_buf[...] = rms(xb[...].astype(F32), gain_row(ag_ref, layer)).astype(BF16)
+            swap = pair_copy(a_buf.at[:, pl.ds(pl.multiple_of(other * half_k, 128), half_k)], a_pair.at[1], 0)
+            swap.start()
+            a_pair[0] = a_buf[:, pl.ds(pl.multiple_of(core * half_k, 128), half_k)]
+            acc_q[...] = jnp.zeros_like(acc_q)
+            swap.wait_recv()
+        with jax.named_scope('dq'):
+            down_project(layer, 2, lambda i: a_pair[:, :, pl.ds(pl.multiple_of(i * kc, 128), kc)].reshape(2 * rows, kc), acc_q)
+        with jax.named_scope('latnorm'):
+            back = pair_copy(acc_q.at[1], acc_in, 1)
+            back.start()
+            back.wait_recv()
+            put_latents(layer, me, acc_q[0] + acc_in[...])
+            swap.wait_send()
+            back.wait_send()
+        with jax.named_scope('agq'):
+            all_gather(q_all, q_specs, lambda j: None)
+
+    def layer_body(layer, carry):
+        more = layer + 1 < layers
         out_c = pltpu.make_async_copy(q_all.at[:, :, pl.ds(lora, latent)], ckv_out.at[layer], out_sem.at[0])
         out_k = pltpu.make_async_copy(q_all.at[:, :, pl.ds(lora + latent, 2 * rope)], kpe_out.at[layer], out_sem.at[1])
         out_c.start()
         out_k.start()
+
+        half_b = batch // 2
+        far_rows = pl.ds(pl.multiple_of(other * half_b, half_b), half_b)
+
+        def head_copy(src, dst, i):
+            return pltpu.make_async_remote_copy(src_ref=src, dst_ref=dst, send_sem=hx_sem.at[0, i], recv_sem=hx_sem.at[1, i],
+                                                device_id={'tp': mate}, device_id_type=MESH)
 
         w_copy(layer, 0).wait()
         c_q = q_all[:, :, pl.ds(0, lora)].reshape(batch, lora)
@@ -378,20 +411,22 @@
             swp = pltpu.roll(duo, rope, 1)
             r_buf[2 * pair_i] = jnp.where(lane2 < rope, duo, swp).astype(BF16)
             r_buf[2 * pair_i + 1] = jnp.where(lane2 < rope, swp, duo).astype(BF16)
+        head_copy(r_buf.at[:, far_rows], r_in, heads).start()
         w_copy(layer, 1).wait()
         wf[...] = uk_buf[...].astype(F32)
         for h in range(heads):
             wk_h = wf[pl.ds(h, latent, stride=heads), :].astype(BF16)
             u_buf[h] = dot_nt(q_n[:, h * nope:(h + 1) * nope], wk_h).astype(BF16)
+            head_copy(u_buf.at[h, far_rows], u_in.at[h], h).start()
 
         @pl.when(more)
         def _():
             w_copy(layer + 1, 0).start()
             w_copy(layer + 1, 1).start()
 
-        m_rows = heads * seqs
-
-        groups = batch // seqs
+        m_rows = 2 * heads * seqs
+        own = heads * seqs
+        groups = half_b // seqs
         row_b = lax.broadcasted_iota(jnp.int32, (m_rows, keys), 0) % seqs
         lane_k = lax.broadcasted_iota(jnp.int32, (m_rows, keys), 1)
         lane_r = lax.broadcasted_iota(jnp.int32, (m_rows, 2 * rope), 1) // rope
@@ -403,9 +438,13 @@
 
         def scores(g):
             slot = lax.rem(g, cslots)
-            r0 = pl.multiple_of(g * seqs, seqs)
-            u_g = u_buf[:, pl.ds(r0, seqs), :].reshape(m_rows, latent)
-            r_g = r_buf[:, pl.ds(r0, seqs), :].reshape(m_rows, 2 * rope).astype(F32)
+            l0 = pl.multiple_of(g * seqs, seqs)
+            r0 = pl.multiple_of(core * half_b + g * seqs, seqs)
+            blk = core * groups + g
+            u_g = jnp.concatenate([u_buf[:, pl.ds(r0, seqs), :].reshape(own, latent),
+                                   u_in[:, pl.ds(l0, seqs), :].reshape(own, latent)], axis=0)
+            r_g = jnp.concatenate([r_buf[:, pl.ds(r0, seqs), :].reshape(own, 2 * rope),
+                                   r_in[:, pl.ds(l0, seqs), :].reshape(own, 2 * rope)], axis=0).astype(F32)
             s_t = dot_nt(u_g, ckv_buf[slot].reshape(seqs * keys, latent))
             s_n = s_t[:, 0:keys]
             for b in range(1, seqs):
@@ -413,26 +452,48 @@
             q_blk = jnp.concatenate(
                 [jnp.where(row_b == 2 * b + lane_r, r_g, 0.0).astype(BF16) for b in range(seqs // 2)], axis=1)
             s_r = dot_nn(q_blk, kpe_buf[slot].reshape(seqs * rope, keys))
-            cn = tile_rows(q_all[g, :, pl.ds(lora, latent)].astype(F32), heads)
-            kn = tile_rows(q_all[g, :, pl.ds(lora + latent, 2 * rope)].astype(F32), heads)
+            cn = tile_rows(q_all[blk, :, pl.ds(lora, latent)].astype(F32), 2 * heads)
+            kn = tile_rows(q_all[blk, :, pl.ds(lora + latent, 2 * rope)].astype(F32), 2 * heads)
             fresh = jnp.sum(u_g.astype(F32) * cn, axis=-1, keepdims=True) + jnp.sum(r_g * kn, axis=-1, keepdims=True)
-            pos = tile_rows(pos_ref[pl.ds(r0, seqs), :], heads)
+            pos = tile_rows(pos_ref[pl.ds(r0, seqs), :], 2 * heads)
             s = jnp.where(lane_k == pos, fresh, s_n + s_r) * scale
             return jnp.where(lane_k <= pos, s, NEG_INF)
 
         def context(g, s):
             slot = lax.rem(g, cslots)
-            r0 = pl.multiple_of(g * seqs, seqs)
+            l0 = pl.multiple_of(g * seqs, seqs)
+            r0 = pl.multiple_of(core * half_b + g * seqs, seqs)
+            blk = core * groups + g
             e = jnp.exp(s - jnp.max(s, axis=-1, keepdims=True))
             prob = (e / jnp.sum(e, axis=-1, keepdims=True)).astype(BF16).astype(F32)
-            at_pos = lane_k == tile_rows(pos_ref[pl.ds(r0, seqs), :], heads)
+            at_pos = lane_k == tile_rows(pos_ref[pl.ds(r0, seqs), :], 2 * heads)
             p_new = jnp.sum(jnp.where(at_pos, prob, 0.0), axis=-1, keepdims=True)
             p_old = jnp.where(at_pos, 0.0, prob)
             p_blk = jnp.concatenate([jnp.where(row_b == b, p_old, 0.0).astype(BF16) for b in range(seqs)], axis=1)
-            cn = tile_rows(q_all[g, :, pl.ds(lora, latent)].astype(F32), heads)
+            cn = tile_rows(q_all[blk, :, pl.ds(lora, latent)].astype(F32), 2 * heads)
             ctx = dot_nn(p_blk, ckv_buf[slot].reshape(seqs * keys, latent)) + p_new * cn
-            ctx_buf[:, pl.ds(r0, seqs), :] = ctx.astype(BF16).reshape(heads, seqs, latent)
-
+            ctx = ctx.astype(BF16)
+            ctx_buf[:, pl.ds(r0, seqs), :] = ctx[:own].reshape(heads, seqs, latent)
+            ctx_out[:, pl.ds(l0, seqs), :] = ctx[own:].reshape(heads, seqs, latent)
+            ctx_copy(g).start()
+
+        def ctx_copy(g):
+            l0 = pl.multiple_of(g * seqs, seqs)
+            r0 = pl.multiple_of(core * half_b + g * seqs, seqs)
+            return pltpu.make_async_remote_copy(
+                src_ref=ctx_out.at[:, pl.ds(l0, seqs)], dst_ref=ctx_buf.at[:, pl.ds(r0, seqs)], send_sem=cx_sem.at[0, g],
+                recv_sem=cx_sem.at[1, g], device_id={'tp': mate}, device_id_type=MESH)
+
+        def ctx_arrival(g):
+            l0 = pl.multiple_of(g * seqs, seqs)
+            r0 = pl.multiple_of(other * half_b + g * seqs, seqs)
+            return pltpu.make_async_remote_copy(
+                src_ref=ctx_out.at[:, pl.ds(l0, seqs)], dst_ref=ctx_buf.at[:, pl.ds(r0, seqs)], send_sem=cx_sem.at[0, g],
+                recv_sem=cx_sem.at[1, g], device_id={'tp': mate}, device_id_type=MESH)
+
+        for h in range(heads):
+            head_copy(u_buf.at[h, far_rows], u_in.at[h], h).wait_recv()
+        head_copy(r_buf.at[:, far_rows], r_in, heads).wait_recv()
         att_wait(0)
         s_buf[...] = scores(0)
 
@@ -458,6 +519,13 @@
                 w_copy(layer, idx).start()
 
         context(groups - 1, s_buf[...])
+        for h in range(heads):
+            head_copy(u_buf.at[h, far_rows], u_in.at[h], h).wait_send()
+        head_copy(r_buf.at[:, far_rows], r_in, heads).wait_send()
+        for g in range(groups):
+            ctx_arrival(g).wait_recv()
+        for g in range(groups):
+            ctx_copy(g).wait_send()
 
         w_copy(layer, 2).wait()
         wf[...] = uv_buf[...].astype(F32)
@@ -512,20 +580,28 @@
         def _():
             w_copy(layer + 1, 6).start()
 
-        rs_drain(final2)
+        def send_rows(j):
+            @pl.when(jnp.logical_not(more))
+            def _():
+                b_all[me, :, pl.ds(j * cw, cw)] = xb[:, pl.ds(j * cw, cw)]
+                ag_first(b_all, j, x_specs[j])
+
+        rs_drain(final2, send_rows)
+
+        @pl.when(more)
+        def _():
+            front(layer + 1)
         return carry
 
     lax.fori_loop(0, layers, layer_body, 0)
 
-    b_all[me] = xb[...]
-
     def put(j):
-        cols = pl.ds(j * gw, gw)
+        cols = pl.ds(j * cw, cw)
         pltpu.make_async_copy(b_all.at[:, :, cols], x_out.at[:, :, cols], out_sem.at[j]).start()
 
-    all_gather(b_all, x_specs, put)
-    for j in range(gchunks):
-        cols = pl.ds(j * gw, gw)
+    all_gather(b_all, x_specs, put, started=True)
+    for j in range(chunks):
+        cols = pl.ds(j * cw, cw)
         pltpu.make_async_copy(b_all.at[:, :, cols], x_out.at[:, :, cols], out_sem.at[j]).wait()
 
 
@@ -568,9 +644,14 @@
             pltpu.VMEM((tp, rows, model), BF16),
             pltpu.VMEM((tp, rows, qw), BF16),
             pltpu.VMEM((2, rows, lora + latent + 2 * rope), F32),
+            pltpu.VMEM((tp, rows, lora + latent + 2 * rope), F32),
+            pltpu.VMEM((tp, rows, lora + latent + 2 * rope), F32),
             pltpu.VMEM((heads, batch, latent), BF16),
             pltpu.VMEM((heads, batch, 2 * rope), BF16),
+            pltpu.VMEM((heads, batch // 2, latent), BF16),
+            pltpu.VMEM((heads, batch // 2, 2 * rope), BF16),
             pltpu.VMEM((heads, batch, latent), BF16),
+            pltpu.VMEM((heads, batch // 2, latent), BF16),
             pltpu.VMEM((batch, heads * nope), BF16),
             pltpu.VMEM((latent * heads, nope), F32),
             pltpu.VMEM((batch, 2 * ffn), F32),
@@ -591,8 +672,8 @@
             pltpu.VMEM((ffn, model), BF16),
             pltpu.VMEM((cslots, seqs, keys, latent), BF16),
             pltpu.VMEM((cslots, seqs, rope, keys), BF16),
-            pltpu.VMEM((heads * seqs, keys), F32),
-            dma(()), dma((5,)), dma((2, 2)), dma((slots,)), dma((slots,)), dma((7,)), dma((2, cslots)), dma((gchunks,)),
+            pltpu.VMEM((2 * heads * seqs, keys), F32),
+            dma((2,)), dma((5,)), dma((2, 3)), dma((2, heads + 1)), dma((2, batch // 2 // seqs)), dma((slots,)), dma((slots,)), dma((7,)), dma((2, cslots)), dma((gchunks,)),
             dma((gchunks, 9)), dma((gchunks, 9)), dma((chunks, 7)), dma((chunks, 7)),
         ]
         cfg = dict(tp=tp, layers=layers, heads=heads, kc=kc, slots=slots, chunks=chunks, seqs=seqs, cslots=cslots, gchunks=gchunks, direct=direct)

time: 161 us -> 152 us (0.944)
  Pallas kernels: 153 us -> 145 us
    pallas_call x1, Pallas kernels: 153 us -> 145 us  [device_body(): call(x_in.reshape(tp, rows, model), pos_ids.reshape(1, batch), attn_gain,...]
where the time goes in v4:
time: 152 us; the launch traced here: 151 us
  Pallas kernels  145 us (95%)
  local copies, waits for them, and re-layouts  6.06 us (4%)
    pallas_call x1, Pallas kernels, device_body(): call(x_in.reshape(tp, rows, model), pos_ids.reshape(1, batch), attn_gain,...  145 us
    unnamed x3, local copies, waits for them, and re-layouts  6.06 us

profile of v4, /device:TPU:113, one launch (start us, length us, event | category | flops | bytes accessed | tf_op | source)
XLA Modules:
  0.0 151.3 jit_solution(14068104473224970890)
XLA Ops:
  0.6 144.6 %decode_step.1 = (bf16[8,16,7168]{2,1,0:T(8,128)(2,1)}, bf16[2,8,16,512]{3,2,1,0:T(8,128)(2,1)}, bf16[2,8,16,128]{3,2,1,0:T(8,128)(2,1)}) custom-call(bf16[8,16,7168]{2,1,0:T(8,128)(2,1)} %bitcast.22, s32[1,128]{1,0:T(1,128)} %bitcast.28, bf16[2,7168]{1,0:T(2,128)(2,1)} %ag_hbm.1, bf16[2,7168]{1,0:T(2,128)(2,1)} %mg_hbm.1, bf16[2,1536]{1,0:T(2,128)(2,1)} %qg_hbm.1, ...), custom_call_target="tpu_custom_call" | custom-call | tf_op jit(solution)/shard_map/decode_step/pallas_call | solution.py:691
  145.2 1.5 %copy.21 = bf16[2,128,64]{1,2,0:T(8,128)(2,1)} copy(bf16[2,128,64]{2,1,0:T(8,128)(2,1)} %bitcast.27) | data formatting | bytes 65536
  146.7 2.8 %copy.24 = bf16[128,7168]{1,0:T(8,128)(2,1)} copy(bf16[128,7168]{1,0:T(8,128)(2,1)} %bitcast.23) | data formatting | bytes 3670016
  149.6 1.7 %copy.25 = bf16[2,128,512]{2,1,0:T(8,128)(2,1)} copy(bf16[2,128,512]{2,1,0:T(8,128)(2,1)} %bitcast.26) | data formatting | bytes 524288

commit v5 on v4

--- a/solution.py
+++ b/solution.py
@@ -44,14 +44,14 @@
                 wdq, wkv, wuq, wuk, wuv, wo, wg, wu, wd, ckv_hbm, kpe_hbm,
                 x_out, ckv_out, kpe_out,
                 pos_row, ag_ref, mg_ref, qg_ref, kg_ref, cos_ref, sin_ref, pos_ref,
-                xb, a_buf, a_pair, acc_in, b_all, q_all, acc_q, acc_all, acc_rcv, u_buf, r_buf, u_in, r_in, ctx_buf, ctx_out, o_buf, wf,
-                gu_acc, act_buf,
-                part, d2d, psum, rel, cmb, fin,
-                dq_buf, kv_buf, uq_buf, uk_buf, uv_buf, wo_buf, wgu_buf, wd_buf, ckv_buf, kpe_buf, s_buf,
+                xb, a_buf, a_pair, b_all, q_all, acc_all, acc_rcv, u_buf, r_buf, u_in, r_in, ctx_buf, ctx_out, o_buf, wf,
+                act_buf,
+                part, d2d, rel, cmb, fin,
+                dq_buf, kv_buf, uq_buf, uk_buf, uv_buf, wo_buf, wgu_buf, wd_buf, ckv_buf, kpe_buf, s_buf, kt_buf,
                 x_sem, s_sem, px_sem, hx_sem, cx_sem, dq_sem, kv_sem, w_sem, c_sem, out_sem,
                 ag_send, ag_recv, rs_send, rs_recv):
-    tp_size, layers, heads, kc, slots, chunks, seqs = (
-        cfg['tp'], cfg['layers'], cfg['heads'], cfg['kc'], cfg['slots'], cfg['chunks'], cfg['seqs'])
+    tp_size, layers, heads, kc, slots, seqs = (
+        cfg['tp'], cfg['layers'], cfg['heads'], cfg['kc'], cfg['slots'], cfg['seqs'])
     nchip = tp_size // 2
     model = xb.shape[1]
     rows = xb.shape[0]
@@ -65,10 +65,14 @@
     cslots = cfg['cslots']
     half_k = model // 2
     n_dq = half_k // kc
-    cw = model // chunks
-    ch = cw // 2
+    widths = cfg['widths']
+    chunks = len(widths)
+    offs = [sum(widths[:j]) for j in range(chunks)]
     scale = float((nope + rope) ** -0.5)
 
+    psum = d2d
+    gu_acc = acc_all.at[:, :, 0:2 * wd_buf.shape[0]]
+    acc_q, acc_in = acc_all.at[0:2], acc_rcv.at[0]
     me = lax.axis_index('tp')
     core = lax.rem(me, 2)
     chip = me // 2
@@ -185,11 +189,8 @@
             forward(j)
             if 1 <= j <= lead:
                 pass_far(j - 1)
-            if 2 <= j <= lead + 1:
-                finish(j - 2)
-        if lead:
-            for j in range(max(n - 2, 0), lead):
-                finish(j)
+        for j in range(lead):
+            finish(j)
         pass_far(lead)
         for j in range(lead, n):
             if j + 1 < n:
@@ -201,10 +202,11 @@
                     ag_desc(buf, j, specs[j], kind, *ag_route(specs[j], kind)).wait_send()
 
     def rs_desc(j, kind):
-        o = j * cw
-        ca, cb = pl.ds(o, ch), pl.ds(o + ch, ch)
-        hj = pl.ds(j * ch, ch)
-        full = pl.ds(o, cw)
+        o, w = offs[j], widths[j]
+        h = w // 2
+        ca, cb = pl.ds(o, h), pl.ds(o + h, h)
+        hj = pl.ds(o // 2, h)
+        full = pl.ds(o, w)
         src, dst, dev = [
             lambda: (part.at[:, other, :, full], d2d.at[:, :, full], mate),
             lambda: (psum.at[ochip, :, ca], rel.at[0, :, hj], right),
@@ -218,13 +220,13 @@
 
     def reduce_scatter(product):
         def mm(j):
-            val = product(j)
-            part[:, :, :, pl.ds(j * cw, cw)] = val.reshape(nchip, 2, rows, cw).astype(BF16)
+            o, w = offs[j], widths[j]
+            part[:, :, :, pl.ds(o, w)] = product(pl.ds(o, w)).reshape(nchip, 2, rows, w).astype(BF16)
             rs_desc(j, 0).start()
 
         def pair(j):
             rs_desc(j, 0).wait_recv()
-            cols = pl.ds(j * cw, cw)
+            cols = pl.ds(offs[j], widths[j])
             psum[ochip, :, cols] = (part[ochip, core, :, cols].astype(F32) + d2d[ochip, :, cols].astype(F32)).astype(BF16)
             rs_desc(j, 1).start()
             rs_desc(j, 2).start()
@@ -232,19 +234,19 @@
                 psum[cc, :, cols] = (part[cc, core, :, cols].astype(F32) + d2d[cc, :, cols].astype(F32)).astype(BF16)
 
         def combine(j):
-            o = j * cw
-            hj = pl.ds(j * ch, ch)
+            o, h = offs[j], widths[j] // 2
+            hj = pl.ds(o // 2, h)
             rs_desc(j, 1).wait_recv()
-            cmb[0, :, hj] = (psum[rchip, :, pl.ds(o, ch)].astype(F32) + rel[0, :, hj].astype(F32)).astype(BF16)
+            cmb[0, :, hj] = (psum[rchip, :, pl.ds(o, h)].astype(F32) + rel[0, :, hj].astype(F32)).astype(BF16)
             rs_desc(j, 5).start()
             rs_desc(j, 2).wait_recv()
-            cmb[1, :, hj] = (psum[lchip, :, pl.ds(o + ch, ch)].astype(F32) + rel[1, :, hj].astype(F32)).astype(BF16)
+            cmb[1, :, hj] = (psum[lchip, :, pl.ds(o + h, h)].astype(F32) + rel[1, :, hj].astype(F32)).astype(BF16)
             rs_desc(j, 6).start()
 
         def final(j):
             for kind in (3, 4, 5, 6):
                 rs_desc(j, kind).wait_recv()
-            cols = pl.ds(j * cw, cw)
+            cols = pl.ds(offs[j], widths[j])
             total = psum[chip, :, cols].astype(F32) + fin[0, :, cols].astype(F32) + fin[1, :, cols].astype(F32)
             xb[:, cols] = (xb[:, cols].astype(F32) + total).astype(BF16)
 
@@ -273,7 +275,7 @@
     gw = model // gchunks
     gh = (gw // 128 + 1) // 2 * 128
     b_specs = [(j * gw, gh, gw, j < cfg['direct']) for j in range(gchunks)]
-    x_specs = [(j * cw, ch, cw, False) for j in range(chunks)]
+    x_specs = [(offs[j], widths[j] // 2, widths[j], False) for j in range(chunks)]
     qw = q_all.shape[2]
     q_specs = [(0, 0, qw, True)]
 
@@ -290,9 +292,70 @@
     x_copy().start()
     for i, (src, dst) in enumerate(small):
         pltpu.make_async_copy(src, dst, s_sem.at[i]).start()
-    start_dq(0)
+    def pair_copy(src, dst, i):
+        return pltpu.make_async_remote_copy(src_ref=src, dst_ref=dst, send_sem=px_sem.at[0, i], recv_sem=px_sem.at[1, i],
+                                            device_id={'tp': mate}, device_id_type=MESH)
+
+    def put_latents(layer, blk, lat):
+        q_all[blk, :, pl.ds(0, lora)] = rms(lat[:, :lora], gain_row(qg_ref, layer)).astype(BF16)
+        kv = lat[:, lora:]
+        q_all[blk, :, pl.ds(lora, latent)] = rms(kv[:, :latent], gain_row(kg_ref, layer)).astype(BF16)
+        row0 = pl.multiple_of(blk * rows, rows)
+        kr = kv[:, latent:latent + rope]
+        kr = jnp.concatenate([kr, kr], axis=1)
+        kr = kr * cos_ref[pl.ds(row0, rows), 0:2 * rope] + swap_halves(kr, rope // 2) * sin_ref[pl.ds(row0, rows), 0:2 * rope]
+        lane = lax.broadcasted_iota(jnp.int32, kr.shape, 1)
+        q_all[blk, :, pl.ds(lora + latent, 2 * rope)] = jnp.where(lane < rope, kr, 0.0).astype(BF16)
+
+    def down_project(layer, blocks, acts, acc):
+        def dq_step(i, c):
+            slot = lax.rem(i, slots)
+            dq_copy(layer, i, slot).wait()
+            kv_copy(layer, i, slot).wait()
+            a_c = acts(i)
+            acc[:, :, 0:lora] += dot_nn(a_c, dq_buf[slot]).reshape(blocks, rows, lora)
+            acc[:, :, lora:lora + latent + rope] += dot_nt(a_c, kv_buf[slot]).reshape(blocks, rows, latent + rope)
+
+            @pl.when(i + slots < n_dq)
+            def _():
+                dq_copy(layer, i + slots, slot).start()
+                kv_copy(layer, i + slots, slot).start()
+            return c
+
+        lax.fori_loop(0, n_dq, dq_step, 0)
+
+    acc_all[...] = jnp.zeros_like(acc_all)
     for i, (src, dst) in enumerate(small):
         pltpu.make_async_copy(src, dst, s_sem.at[i]).wait()
+    x_all.wait()
+    start_dq(0)
+    x_copy().wait()
+    my_half = pl.ds(pl.multiple_of(core * half_k, 128), half_k)
+    gain_0 = ag_ref[0:1, :].astype(F32)
+    gain_h = jnp.where(core == 0, gain_0[:, :half_k], gain_0[:, half_k:])
+
+    def norm_block(i, c):
+        vals = b_all[i].astype(F32)
+        inv = lax.rsqrt(jnp.mean(vals * vals, axis=-1, keepdims=True) + NORM_EPS)
+        b_all[i, :, my_half] = (b_all[i, :, my_half].astype(F32) * inv * gain_h).astype(BF16)
+        return c
+
+    lax.fori_loop(0, tp_size, norm_block, 0)
+    down_project(0, tp_size, lambda i: b_all[:, :, pl.ds(pl.multiple_of(core * half_k + i * kc, 128), kc)].reshape(batch, kc), acc_all)
+    for idx in (0, 1, 2):
+        w_copy(0, idx).start()
+    start_cache(0)
+    w_copy(0, 3).start()
+    pl.semaphore_wait(barrier, 4)
+    pieces = 4
+    per_piece = tp_size // pieces
+
+    def piece(i):
+        blks = pl.ds(i * per_piece, per_piece)
+        return pair_copy(acc_all.at[blks], acc_rcv.at[blks], 2 + i)
+
+    for i in range(pieces):
+        piece(i).start()
     pos_f = jnp.transpose(jnp.broadcast_to(pos_row[...].astype(F32), (batch, batch)))
     pos_ref[...] = pos_f.astype(jnp.int32)
     lane_f = lax.broadcasted_iota(jnp.int32, (batch, batch), 1) % (rope // 2)
@@ -303,65 +366,16 @@
     for i in range(heads * rope // batch):
         cos_ref[:, i * batch:(i + 1) * batch] = cos_v
         sin_ref[:, i * batch:(i + 1) * batch] = sin_v
-    x_copy().wait()
-
-    def pair_copy(src, dst, i):
-        return pltpu.make_async_remote_copy(src_ref=src, dst_ref=dst, send_sem=px_sem.at[0, i], recv_sem=px_sem.at[1, i],
-                                            device_id={'tp': mate}, device_id_type=MESH)
-
-    def put_latents(layer, blk, lat):
-        q_all[blk, :, pl.ds(0, lora)] = rms(lat[:, :lora], gain_row(qg_ref, layer)).astype(BF16)
-        kv = lat[:, lora:]
-        q_all[blk, :, pl.ds(lora, latent)] = rms(kv[:, :latent], gain_row(kg_ref, layer)).astype(BF16)
-        row0 = pl.multiple_of(blk * rows, rows)
-        kr = kv[:, latent:latent + rope]
-        kr = jnp.concatenate([kr, kr], axis=1)
-        kr = kr * cos_ref[pl.ds(row0, rows), 0:2 * rope] + swap_halves(kr, rope // 2) * sin_ref[pl.ds(row0, rows), 0:2 * rope]
-        lane = lax.broadcasted_iota(jnp.int32, kr.shape, 1)
-        q_all[blk, :, pl.ds(lora + latent, 2 * rope)] = jnp.where(lane < rope, kr, 0.0).astype(BF16)
-
-    def down_project(layer, blocks, acts, acc):
-        def dq_step(i, c):
-            slot = lax.rem(i, slots)
-            dq_copy(layer, i, slot).wait()
-            kv_copy(layer, i, slot).wait()
-            a_c = acts(i)
-            acc[:, :, 0:lora] += dot_nn(a_c, dq_buf[slot]).reshape(blocks, rows, lora)
-            acc[:, :, lora:lora + latent + rope] += dot_nt(a_c, kv_buf[slot]).reshape(blocks, rows, latent + rope)
-
-            @pl.when(i + slots < n_dq)
-            def _():
-                dq_copy(layer, i + slots, slot).start()
-                kv_copy(layer, i + slots, slot).start()
-            return c
-
-        lax.fori_loop(0, n_dq, dq_step, 0)
-
-    x_all.wait()
-    gain_0 = ag_ref[0:1, :].astype(F32)
-
-    def norm_block(i, c):
-        b_all[i] = rms(b_all[i].astype(F32), gain_0).astype(BF16)
-        return c
-
-    lax.fori_loop(0, tp_size, norm_block, 0)
-    acc_all[...] = jnp.zeros_like(acc_all)
-    down_project(0, tp_size, lambda i: b_all[:, :, pl.ds(pl.multiple_of(core * half_k + i * kc, 128), kc)].reshape(batch, kc), acc_all)
-    for idx in (0, 1, 2):
-        w_copy(0, idx).start()
-    start_cache(0)
-    w_copy(0, 3).start()
-    pl.semaphore_wait(barrier, 4)
-    whole = pair_copy(acc_all, acc_rcv, 2)
-    whole.start()
-    whole.wait_recv()
 
     def latent_block(i, c):
         put_latents(0, i, acc_all[i] + acc_rcv[i])
         return c
 
-    lax.fori_loop(0, tp_size, latent_block, 0)
-    whole.wait_send()
+    for i in range(pieces):
+        piece(i).wait_recv()
+        lax.fori_loop(i * per_piece, (i + 1) * per_piece, latent_block, 0)
+    for i in range(pieces):
+        piece(i).wait_send()
 
     def front(layer):
         with jax.named_scope('norm'):
@@ -369,7 +383,7 @@
             swap = pair_copy(a_buf.at[:, pl.ds(pl.multiple_of(other * half_k, 128), half_k)], a_pair.at[1], 0)
             swap.start()
             a_pair[0] = a_buf[:, pl.ds(pl.multiple_of(core * half_k, 128), half_k)]
-            acc_q[...] = jnp.zeros_like(acc_q)
+            acc_q[...] = jnp.zeros(acc_q.shape, F32)
             swap.wait_recv()
         with jax.named_scope('dq'):
             down_project(layer, 2, lambda i: a_pair[:, :, pl.ds(pl.multiple_of(i * kc, 128), kc)].reshape(2 * rows, kc), acc_q)
@@ -386,7 +400,9 @@
     def layer_body(layer, carry):
         more = layer + 1 < layers
         out_c = pltpu.make_async_copy(q_all.at[:, :, pl.ds(lora, latent)], ckv_out.at[layer], out_sem.at[0])
-        out_k = pltpu.make_async_copy(q_all.at[:, :, pl.ds(lora + latent, 2 * rope)], kpe_out.at[layer], out_sem.at[1])
+        kpe_t = jnp.transpose(q_all[:, :, pl.ds(lora + latent, 2 * rope)].astype(F32).reshape(batch, 2 * rope))
+        kt_buf[...] = kpe_t[0:rope].astype(BF16)
+        out_k = pltpu.make_async_copy(kt_buf, kpe_out.at[layer], out_sem.at[1])
         out_c.start()
         out_k.start()
 
@@ -503,12 +519,6 @@
             s_next = scores(g + 1)
             context(g, s_now)
             s_buf[...] = s_next
-
-            @pl.when(g + cslots < groups)
-            def _():
-                slot = lax.rem(g, cslots)
-                ckv_copy(layer, g + cslots, slot).start()
-                kpe_copy(layer, g + cslots, slot).start()
             return c
 
         lax.fori_loop(0, groups - 1, att_step, 0)
@@ -522,13 +532,12 @@
         for h in range(heads):
             head_copy(u_buf.at[h, far_rows], u_in.at[h], h).wait_send()
         head_copy(r_buf.at[:, far_rows], r_in, heads).wait_send()
+        w_copy(layer, 2).wait()
+        wf[...] = uv_buf[...].astype(F32)
         for g in range(groups):
             ctx_arrival(g).wait_recv()
         for g in range(groups):
             ctx_copy(g).wait_send()
-
-        w_copy(layer, 2).wait()
-        wf[...] = uv_buf[...].astype(F32)
         for h in range(heads):
             wv_h = wf[pl.ds(h, latent, stride=heads), :].astype(BF16)
             o_buf[:, h * nope:(h + 1) * nope] = dot_nn(ctx_buf[h], wv_h).astype(BF16)
@@ -541,7 +550,7 @@
         out_c.wait()
         out_k.wait()
 
-        final = reduce_scatter(lambda j: dot_nn(o_buf[...], wo_buf[:, pl.ds(j * cw, cw)]))
+        final = reduce_scatter(lambda cols: dot_nn(o_buf[...], wo_buf[:, cols]))
 
         @pl.when(more)
         def _():
@@ -558,15 +567,16 @@
         def gate_up(j):
             cols = pl.ds(j * gw, gw)
             b_c = b_all[:, :, cols].reshape(batch, gw)
-            val = dot_nt(b_c, wgu_buf[:, cols])
+            val = dot_nt(b_c, wgu_buf[:, cols]).reshape(tp_size, rows, 2 * ffn)
             if j == 0:
                 gu_acc[...] = val
             else:
                 gu_acc[...] += val
 
         all_gather(b_all, b_specs, gate_up)
-        gate = gu_acc[:, 0:ffn]
-        act_buf[...] = (gate * lax.logistic(gate) * gu_acc[:, ffn:2 * ffn]).astype(BF16)
+        both = gu_acc[...].reshape(batch, 2 * ffn)
+        gate = both[:, 0:ffn]
+        act_buf[...] = (gate * lax.logistic(gate) * both[:, ffn:2 * ffn]).astype(BF16)
         w_copy(layer, 6).wait()
 
         @pl.when(more)
@@ -574,7 +584,7 @@
             w_copy(layer + 1, 4).start()
             w_copy(layer + 1, 5).start()
 
-        final2 = reduce_scatter(lambda j: dot_nn(act_buf[...], wd_buf[:, pl.ds(j * cw, cw)]))
+        final2 = reduce_scatter(lambda cols: dot_nn(act_buf[...], wd_buf[:, cols]))
 
         @pl.when(more)
         def _():
@@ -583,7 +593,7 @@
         def send_rows(j):
             @pl.when(jnp.logical_not(more))
             def _():
-                b_all[me, :, pl.ds(j * cw, cw)] = xb[:, pl.ds(j * cw, cw)]
+                b_all[me, :, pl.ds(offs[j], widths[j])] = xb[:, pl.ds(offs[j], widths[j])]
                 ag_first(b_all, j, x_specs[j])
 
         rs_drain(final2, send_rows)
@@ -596,13 +606,29 @@
     lax.fori_loop(0, layers, layer_body, 0)
 
     def put(j):
-        cols = pl.ds(j * cw, cw)
+        cols = pl.ds(offs[j], widths[j])
         pltpu.make_async_copy(b_all.at[:, :, cols], x_out.at[:, :, cols], out_sem.at[j]).start()
 
     all_gather(b_all, x_specs, put, started=True)
     for j in range(chunks):
-        cols = pl.ds(j * cw, cw)
+        cols = pl.ds(offs[j], widths[j])
         pltpu.make_async_copy(b_all.at[:, :, cols], x_out.at[:, :, cols], out_sem.at[j]).wait()
+
+
+def copy_kernel(split, x_in, c_in, k_in, x_out, c_out, k_out, x_buf, c_buf, k_buf, in_sem, out_sem):
+    size = x_in.shape[0] // split
+    parts = [(x_in.at[i * size:(i + 1) * size], x_buf.at[i * size:(i + 1) * size], x_out.at[i * size:(i + 1) * size])
+             for i in range(split)]
+    parts += [(c_in, c_buf, c_out), (k_in, k_buf, k_out)]
+    loads = [pltpu.make_async_copy(src, buf, in_sem.at[i]) for i, (src, buf, _) in enumerate(parts)]
+    stores = [pltpu.make_async_copy(buf, dst, out_sem.at[i]) for i, (_, buf, dst) in enumerate(parts)]
+    for load in loads:
+        load.start()
+    for load, store in zip(loads, stores):
+        load.wait()
+        store.start()
+    for store in stores:
+        store.wait()
 
 
 def solution(mesh):
@@ -623,11 +649,12 @@
         nope = w_uk.shape[-1]
         ffn = w_gate.shape[-1]
         rows = batch // tp
-        kc, slots, chunks, gchunks, direct, seqs, cslots = 512, 3, 4, 4, 1, rows, 3
+        kc, slots, gchunks, direct, seqs, cslots = 512, 3, 4, 0, rows, batch // 2 // rows
+        widths = [model * part_w // 28 for part_w in (3, 7, 7, 7, 4)]
+        chunks = len(widths)
         hb = pl.BlockSpec(memory_space=pl.ANY)
         dma = pltpu.SemaphoreType.DMA
         qw = lora + latent + 2 * rope
-        ch = model // chunks // 2
         scratch = [
             pltpu.VMEM((1, batch), jnp.int32),
             pltpu.VMEM((layers, model), BF16),
@@ -640,10 +667,8 @@
             pltpu.VMEM((rows, model), BF16),
             pltpu.VMEM((rows, model), BF16),
             pltpu.VMEM((2, rows, model // 2), BF16),
-            pltpu.VMEM((rows, lora + latent + 2 * rope), F32),
             pltpu.VMEM((tp, rows, model), BF16),
             pltpu.VMEM((tp, rows, qw), BF16),
-            pltpu.VMEM((2, rows, lora + latent + 2 * rope), F32),
             pltpu.VMEM((tp, rows, lora + latent + 2 * rope), F32),
             pltpu.VMEM((tp, rows, lora + latent + 2 * rope), F32),
             pltpu.VMEM((heads, batch, latent), BF16),
@@ -654,10 +679,8 @@
             pltpu.VMEM((heads, batch // 2, latent), BF16),
             pltpu.VMEM((batch, heads * nope), BF16),
             pltpu.VMEM((latent * heads, nope), F32),
-            pltpu.VMEM((batch, 2 * ffn), F32),
             pltpu.VMEM((batch, ffn), BF16),
             pltpu.VMEM((tp // 2, 2, rows, model), BF16),
-            pltpu.VMEM((tp // 2, rows, model), BF16),
             pltpu.VMEM((tp // 2, rows, model), BF16),
             pltpu.VMEM((2, rows, model // 2), BF16),
             pltpu.VMEM((2, rows, model // 2), BF16),
@@ -673,15 +696,16 @@
             pltpu.VMEM((cslots, seqs, keys, latent), BF16),
             pltpu.VMEM((cslots, seqs, rope, keys), BF16),
             pltpu.VMEM((2 * heads * seqs, keys), F32),
-            dma((2,)), dma((5,)), dma((2, 3)), dma((2, heads + 1)), dma((2, batch // 2 // seqs)), dma((slots,)), dma((slots,)), dma((7,)), dma((2, cslots)), dma((gchunks,)),
-            dma((gchunks, 9)), dma((gchunks, 9)), dma((chunks, 7)), dma((chunks, 7)),
+            pltpu.VMEM((rope, batch), BF16),
+            dma((2,)), dma((5,)), dma((2, 6)), dma((2, heads + 1)), dma((2, batch // 2 // seqs)), dma((slots,)), dma((slots,)), dma((7,)), dma((2, cslots)), dma((max(gchunks, chunks),)),
+            dma((max(gchunks, chunks), 9)), dma((max(gchunks, chunks), 9)), dma((chunks, 7)), dma((chunks, 7)),
         ]
-        cfg = dict(tp=tp, layers=layers, heads=heads, kc=kc, slots=slots, chunks=chunks, seqs=seqs, cslots=cslots, gchunks=gchunks, direct=direct)
+        cfg = dict(tp=tp, layers=layers, heads=heads, kc=kc, slots=slots, widths=widths, seqs=seqs, cslots=cslots, gchunks=gchunks, direct=direct)
         call = pl.pallas_call(
             functools.partial(step_kernel, cfg),
             out_shape=(jax.ShapeDtypeStruct((tp, rows, model), BF16),
                        jax.ShapeDtypeStruct((layers, tp, rows, latent), BF16),
-                       jax.ShapeDtypeStruct((layers, tp, rows, 2 * rope), BF16)),
+                       jax.ShapeDtypeStruct((layers, rope, batch), BF16)),
             in_specs=[hb] * 17,
             out_specs=(hb, hb, hb),
             scratch_shapes=scratch,
@@ -695,7 +719,15 @@
             w_o.reshape(layers, heads * nope, model),
             w_gate.transpose(0, 2, 1), w_up.transpose(0, 2, 1), w_down,
             ckv_cache, kpe_cache.transpose(0, 1, 3, 2))
-        return (x_o.reshape(batch, model), c_o.reshape(layers, batch, latent),
-                k_o.reshape(layers, batch, 2 * rope)[..., :rope])
+        split = 4
+        x_o, c_o, k_o = pl.pallas_call(
+            functools.partial(copy_kernel, split),
+            out_shape=tuple(jax.ShapeDtypeStruct(v.shape, v.dtype) for v in (x_o, c_o, k_o)),
+            in_specs=[hb] * 3,
+            out_specs=(hb, hb, hb),
+            scratch_shapes=[pltpu.VMEM(v.shape, v.dtype) for v in (x_o, c_o, k_o)] + [dma((split + 2,)), dma((split + 2,))],
+            name='copy_out',
+        )(x_o, c_o, k_o)
+        return x_o.reshape(batch, model), c_o.reshape(layers, batch, latent), k_o.transpose(0, 2, 1)
 
     return jax.shard_map(device_body, mesh=mesh, in_specs=in_specs, out_specs=out_specs, check_vma=False)

time: 152 us -> 144 us (0.947)
  local copies, waits for them, and re-layouts: 6.06 us -> 0 us
  Pallas kernels: 145 us -> 143 us
    unnamed x3 -> x0, local copies, waits for them, and re-layouts: 6.06 us -> none
    pallas_call x1, Pallas kernels: 145 us -> 140 us  [device_body(): call(x_in.reshape(tp, rows, model), pos_ids.reshape(1, batch), attn_gain,...]
    pallas_call x0 -> x1, Pallas kernels: none -> 2.43 us  [device_body(): pl.pallas_call(functools.partial(copy_kernel, split), out_shape=tuple((ja...]
where the time goes in v5:
time: 144 us; the launch traced here: 143 us
  Pallas kernels  143 us (99%)
    pallas_call x1, Pallas kernels, device_body(): call(x_in.reshape(tp, rows, model), pos_ids.reshape(1, batch), attn_gain,...  140 us

profile of v5, /device:TPU:113, one launch (start us, length us, event | category | flops | bytes accessed | tf_op | source)
XLA Modules:
  0.0 143.5 jit_solution(10899874387904754456)
XLA Ops:
  0.6 140.4 %decode_step.1 = (bf16[8,16,7168]{2,1,0:T(8,128)(2,1)}, bf16[2,8,16,512]{3,2,1,0:T(8,128)(2,1)}, bf16[2,64,128]{2,1,0:T(8,128)(2,1)}) custom-call(bf16[8,16,7168]{2,1,0:T(8,128)(2,1)} %bitcast.21, s32[1,128]{1,0:T(1,128)} %bitcast.24, bf16[2,7168]{1,0:T(2,128)(2,1)} %ag_hbm.1, bf16[2,7168]{1,0:T(2,128)(2,1)} %mg_hbm.1, bf16[2,1536]{1,0:T(2,128)(2,1)} %qg_hbm.1, ...), custom_call_target="tpu_custom_call" | custom-call | tf_op jit(solution)/shard_map/decode_step/pallas_call | solution.py:715
  141.0 2.4 %copy_out.1 = (bf16[8,16,7168]{2,1,0:T(8,128)(2,1)}, bf16[2,8,16,512]{3,2,1,0:T(8,128)(2,1)}, bf16[2,64,128]{2,1,0:T(8,128)(2,1)}) custom-call(bf16[8,16,7168]{2,1,0:T(8,128)(2,1)} %get-tuple-element.9.x_in, bf16[2,8,16,512]{3,2,1,0:T(8,128)(2,1)} %get-tuple-element.10.c_in, bf16[2,64,128]{2,1,0:T(8,128)(2,1)} %get-tuple-element.11.k_in), custom_call_target="tpu_custom_call" | custom-call | tf_op jit(solution)/shard_map/copy_out/pallas_call | solution.py:723
